TPU v7x, 256 devices: a whole 4x4x8 slice. The times are simulated.
256 devices in a mesh: tm: 8 (over z), sub: 32 (over y, x, core).
Axes of the slice: x: 4, y: 4, z: 8, core: 2. Of those that a mesh axis runs over, the one named last changes fastest.
Arguments:
- starts: float32 [8, 32, 16, 1024], P('tm', 'sub'), may hold values from -6 to 6
- inverses: float32 [32, 1024, 1024], P('sub')
- retain: float32 [32, 1024], P('sub'), may hold values from 0.4 to 1.1
- sources: float32 [32, 16, 1024], P('sub'), may hold values from -4 to 4
- coarse_decay: float32 [32, 1024], P('sub'), may hold values from 0.88 to 0.995
- admittance: float32 [32, 8], P('sub'), may hold values from 0.2 to 0.6
- partner: int32 [32, 8], P('sub'), may hold values from 0 to 255, as said below
- line_delay: int32 [32, 8], P('sub'), may hold values from 2 to 5, as said below
- line_live: int32 [32, 8], P('sub'), may hold values from 0 to 1, as said below
- term_block: int32 [32, 8], P('sub'), may hold values from 0 to 127, as said below
Outputs:
- ends: float32 [8, 32, 16, 1024], P('tm', 'sub')
Inputs may be any that keep to these rules, and one draw needn't show every extreme that they name: Slots are paired: partner[i] = k exactly when partner[k] = i. A slot may be its own partner; such a slot is out of service. Of the slots of one index d of sub (its 1 subnetworks), exactly 1 are their own partners, and the others have partners on exactly 7 other indices, 1 slots on each and none elsewhere; these indices are d + 16 and pairs d + s and d - s modulo the number of indices. `line_delay`: paired slots have equal delays. `line_live`: paired slots are both in service or both not. `term_block`: the slots of one subnetwork have distinct blocks.
All inputs are finite; a program needn't handle non-finite values.
Results may differ from a plain program's by a relative error of at most 0.0001.
Values sent between devices are 32-bit elements; how exact they have to be, the bound alone decides.
A program may use at most 64 MiB of HBM per device.

v0:
```python
import jax
import jax.numpy as jnp
from jax import lax
from jax.sharding import PartitionSpec as P

TERM = 8
DMIN = 2
FINE = 4


def joined_along(tiles, dim):
    tiles = jnp.moveaxis(tiles, 0, dim)
    shape = tiles.shape
    return tiles.reshape(*shape[:dim], shape[dim] * shape[dim + 1], *shape[dim + 2 :])


def sent_to_all(shard, axis):
    count = lax.axis_size(axis)
    return lax.all_to_all(
        jnp.broadcast_to(shard[None], (count, *shard.shape)), axis, 0, 0, tiled=True
    )


def collect(shard, axis, dim):
    return joined_along(sent_to_all(shard, axis), dim)


def all_in_one(shard, axis):
    leaves = jax.tree.leaves(shard)
    turns = sorted(range(len(leaves)), key=lambda k: -leaves[k].size)
    width = (1, *leaves[turns[0]].shape)[-1]
    lines = [
        jnp.pad(leaves[k].reshape(-1), (0, -leaves[k].size % width)).reshape(-1, width)
        for k in turns
    ]
    both, at, found = (lax.all_gather(jnp.concatenate(lines), axis), 0, {})
    for k, line in zip(turns, lines):
        piece = both[:, at : at + len(line)].reshape(len(both), -1)
        found[k] = piece[:, : leaves[k].size].reshape(-1, *leaves[k].shape)
        at += len(line)
    numbers = iter(range(len(leaves)))
    return jax.tree.map(lambda _: found[next(numbers)], shard)


def prefix(part, axis, combine, identity):
    place = lax.axis_index(axis)
    gathered = all_in_one(part, axis)
    state = jax.tree.map(lambda a, e: jnp.zeros_like(a) + jnp.asarray(e, a.dtype), part, identity)

    def one(step, state):
        return combine(
            state, jax.tree.map(lambda a: lax.dynamic_index_in_dim(a, step, 0, False), gathered)
        )

    return lax.fori_loop(0, place, one, state)


def terminals(state, term_block):
    grouped = state.reshape(
        state.shape[0], state.shape[1], state.shape[2], state.shape[3] // TERM, TERM
    )
    target = (state.shape[0], state.shape[1], state.shape[2], term_block.shape[1], TERM)
    picked = jnp.take_along_axis(
        grouped, jnp.broadcast_to(term_block[None, :, None, :, None], target), axis=3
    )
    picked = jnp.transpose(picked, (1, 3, 0, 2, 4))
    return picked.reshape(
        picked.shape[0] * picked.shape[1], picked.shape[2], picked.shape[3] * TERM
    )


def inject(collected, source_rows, line_delay, line_live, admittance, term_block, step, state):
    reach = jnp.maximum(step + 1 - line_delay, 0).reshape(-1)
    stacked = jnp.concatenate(collected, axis=0)
    everyone = collected[0].shape[0]
    row_index = reach * everyone + source_rows
    far_values = stacked[row_index]
    far_values = far_values.reshape(
        term_block.shape[0], term_block.shape[1], state.shape[0], state.shape[2], TERM
    )
    weights = admittance * line_live.astype(jnp.float32)
    far_values = far_values * weights[:, :, None, None, None]
    blocks_here = jnp.arange(state.shape[3] // TERM, dtype=jnp.int32)
    onehot = (term_block[:, :, None] == blocks_here[None, None, :]).astype(jnp.float32)
    placed = jnp.einsum("plsct,plb->spcbt", far_values, onehot, precision=lax.Precision.HIGHEST)
    return placed.reshape(state.shape)


def advance(state, inverses, retain, sources, injected):
    driven = retain[None, :, None, :] * state + sources[None] + injected
    return jnp.einsum(
        "spcm,pnm->spcn",
        driven,
        inverses,
        precision=lax.Precision.HIGHEST,
        preferred_element_type=jnp.float32,
    )


def publish(pending, collected):
    stacked = jnp.stack(pending, axis=1)
    arrived = collect(stacked, "sub", 0)
    return collected + [arrived[:, place] for place in range(len(pending))]


def compose(earlier, latter):
    return (latter[0] * earlier[0], latter[0] * earlier[1] + latter[1])


def shards(
    starts,
    inverses,
    retain,
    sources,
    coarse_decay,
    admittance,
    partner,
    line_delay,
    line_live,
    term_block,
):
    source_rows = partner.reshape(-1)
    state = starts
    collected = publish([terminals(state, term_block)], [])
    pending = []
    for step in range(FINE):
        injected = inject(
            collected, source_rows, line_delay, line_live, admittance, term_block, step, state
        )
        state = advance(state, inverses, retain, sources, injected)
        if step + 1 <= FINE - DMIN:
            pending.append(terminals(state, term_block))
            if len(pending) == DMIN or step + 1 == FINE - DMIN:
                collected = publish(pending, collected)
                pending = []
    decay = coarse_decay[:, None, :]
    offsets = state - decay[None] * starts
    combined = offsets[0]
    leading = lax.axis_index("tm") == 0
    head_factor = jnp.where(leading, jnp.zeros_like(decay), decay)
    head_offset = jnp.where(leading, decay * starts[0] + combined, combined)
    prior = prefix(
        (head_factor, head_offset), "tm", compose, (jnp.ones_like(decay), jnp.zeros_like(combined))
    )
    entering = jnp.where(leading, starts[0], prior[1])
    current = entering
    current = decay * current + offsets[0]
    finals = [current]
    return jnp.stack(finals)


def solution(mesh):
    return jax.shard_map(
        shards,
        mesh=mesh,
        in_specs=(
            P("tm", "sub", None, None),
            P("sub", None, None),
            P("sub", None),
            P("sub", None, None),
            P("sub", None),
            P("sub", None),
            P("sub", None),
            P("sub", None),
            P("sub", None),
            P("sub", None),
        ),
        out_specs=P("tm", "sub", None, None),
        check_vma=False,
    )
```

profile of v0, /device:TPU:32, one launch (start us, length us, event | category | flops | bytes accessed | tf_op | source)
XLA Modules:
  0.0 120.5 jit_solution(11359132914212634982)
XLA Ops:
  0.0 0.7 broadcast_add_fusion
  0.7 0.7 broadcast_compare_fusion
  1.3 0.7 fusion.40
  2.1 0.1 reshape.675
  2.1 1.0 copy.48
  3.2 1.0 copy.49
  4.2 0.0 copy-start.7
  4.3 0.0 copy-start.8
  4.3 0.0 copy-start.2
  4.3 9.0 %gather_fusion.4 = f32[1024]{0:T(1024)S(1)} fusion(f32[16,128,8]{2,1,0:T(8,128)S(1)} %bitcast.268, s32[1024]{0:T(1024)S(1)} %reshape.675), kind=kCustom, calls=%fused_computation.clone | custom fusion | bytes 20480 | tf_op jit(solution)/shard_map/jit(take_along_axis)/gather | solution.py:63
  13.3 0.1 reshape.678
  13.4 0.1 select_bitcast_fusion.2
  13.5 0.1 broadcast_in_dim.23
  13.6 0.7 broadcast_in_dim.24
  14.3 7.3 %all-to-all-start = ((f32[32,8,1,1,128]{4,1,3,2,0:T(8,128)}), f32[32,8,1,1,128]{4,1,3,2,0:T(8,128)S(1)}, u32[]{:S(2)}, u32[]{:S(2)}) async-start(f32[32,8,1,1,128]{4,1,3,2,0:T(8,128)} %broadcast_in_dim.24), calls=%async_computation | async-start | bytes 262144 | tf_op jit(solution)/shard_map/all_to_all | solution.py:19
  21.7 7.7 %all-to-all-done = f32[32,8,1,1,128]{4,1,3,2,0:T(8,128)S(1)} async-done(((f32[32,8,1,1,128]{4,1,3,2,0:T(8,128)}), f32[32,8,1,1,128]{4,1,3,2,0:T(8,128)S(1)}, u32[]{:S(2)}, u32[]{:S(2)}) %all-to-all-start) | async-done | bytes 131104 | tf_op jit(solution)/shard_map/all_to_all | solution.py:19
  29.4 0.6 gather_fusion.1
  29.9 0.6 gather_fusion
  30.5 0.1 bitcast_multiply_fusion.7
  30.6 0.1 mul.240
  30.6 0.1 copy.51
  30.7 0.3 convolution_bitcast_fusion.3
  31.0 0.2 copy.52
  31.3 0.2 copy.53
  31.4 0.1 mul.244
  31.5 0.1 copy.54
  31.6 0.3 convolution_bitcast_fusion.2
  31.9 0.2 copy.55
  32.2 0.2 copy.56
  32.3 0.0 copy-done.4
  32.4 5.7 %fusion.8 = f32[1,1,16,1024]{3,2,0,1:T(8,128)S(1)} fusion(f32[1,1024,1024]{2,1,0:T(8,128)} %param.15, f32[1,1,16,1024]{3,2,0,1:T(8,128)S(1)} %copy.53, f32[1,16,1024]{2,1,0:T(8,128)S(1)} %copy-done.2, f32[1,1,16,1024]{3,2,1,0:T(8,128)S(1)} %copy-done.1, f32[1024]{0:T(1024)S(1)} %bitcast.284), kind=kOutput, calls=%fused_computation.21 | convolution fusion | flops 201375744 | bytes 4460544 | tf_op jit(solution)/shard_map/spcm,pnm->spcn/dot_general | solution.py:91
  38.0 0.2 copy.57
  38.2 5.7 %fusion.11 = f32[1,1,16,1024]{3,2,0,1:T(8,128)S(1)} fusion(f32[1,1024,1024]{2,1,0:T(8,128)} %param.15, f32[1,1,16,1024]{3,2,0,1:T(8,128)S(1)} %copy.56, f32[1,16,1024]{2,1,0:T(8,128)S(1)} %copy-done.2, f32[1,1,16,1024]{3,2,0,1:T(8,128)S(1)} %fusion.8, f32[1024]{0:T(1024)S(1)} %bitcast.285), kind=kOutput, calls=%fused_computation.22 | convolution fusion | flops 201375744 | bytes 4460544 | tf_op jit(solution)/shard_map/spcm,pnm->spcn/dot_general | solution.py:91
  43.9 0.2 copy.60
  44.1 1.0 copy.61
  45.2 9.0 %gather_fusion.6 = f32[1024]{0:T(1024)S(1)} fusion(f32[16,128,8]{2,1,0:T(8,128)S(1)} %bitcast.269, s32[1024]{0:T(1024)S(1)} %reshape.675), kind=kCustom, calls=%fused_computation.2.clone | custom fusion | bytes 20480 | tf_op jit(solution)/shard_map/jit(take_along_axis)/gather | solution.py:63
  54.2 0.1 reshape.690
  54.2 1.0 copy.58
  55.3 9.0 %gather_fusion.5 = f32[1024]{0:T(1024)S(1)} fusion(f32[16,128,8]{2,1,0:T(8,128)S(1)} %bitcast.267, s32[1024]{0:T(1024)S(1)} %reshape.675), kind=kCustom, calls=%fused_computation.1.clone | custom fusion | bytes 20480 | tf_op jit(solution)/shard_map/jit(take_along_axis)/gather | solution.py:63
  64.3 0.1 reshape.684
  64.4 0.1 select_bitcast_fusion.1
  64.5 0.1 stack_reshape.6
  64.6 0.1 stack_reshape.7
  64.7 0.7 broadcast_in_dim.26
  65.4 4.0 %all-to-all-start.1 = ((f32[32,8,2,1,128]{4,1,2,3,0:T(8,128)}), f32[32,8,2,1,128]{4,1,2,3,0:T(8,128)S(1)}, u32[]{:S(2)}, u32[]{:S(2)}) async-start(f32[32,8,2,1,128]{4,1,2,3,0:T(8,128)} %broadcast_in_dim.26), calls=%async_computation.1 | async-start | bytes 524288 | tf_op jit(solution)/shard_map/all_to_all | solution.py:19
  69.5 8.7 %all-to-all-done.1 = f32[32,8,2,1,128]{4,1,2,3,0:T(8,128)S(1)} async-done(((f32[32,8,2,1,128]{4,1,2,3,0:T(8,128)}), f32[32,8,2,1,128]{4,1,2,3,0:T(8,128)S(1)}, u32[]{:S(2)}, u32[]{:S(2)}) %all-to-all-start.1) | async-done | bytes 262176 | tf_op jit(solution)/shard_map/all_to_all | solution.py:19
  78.3 0.6 gather_fusion.3
  78.9 0.6 gather_fusion.2
  79.5 0.1 bitcast_multiply_fusion.5
  79.5 0.1 mul.248
  79.6 0.1 copy.64
  79.7 0.3 convolution_bitcast_fusion.1
  80.0 0.2 copy.65
  80.3 0.2 copy.66
  80.4 0.1 mul.253
  80.5 0.1 copy.67
  80.6 0.3 convolution_bitcast_fusion
  80.9 0.2 copy.68
  81.1 0.2 copy.69
  81.3 5.8 %fusion.35 = f32[16,1024]{1,0:T(8,128)S(1)} fusion(f32[1,1,16,1024]{3,2,0,1:T(8,128)S(1)} %copy.69, f32[1,1024,1024]{2,1,0:T(8,128)} %param.15, f32[1,16,1024]{2,1,0:T(8,128)S(1)} %copy-done.2, f32[1,1,16,1024]{3,2,0,1:T(8,128)S(1)} %copy.66, f32[1,1,16,1024]{3,2,0,1:T(8,128)S(1)} %fusion.11, f32[1024]{0:T(1024)S(1)} %bitcast.286), kind=kOutput, calls=%fused_computation.30 | convolution fusion | flops 201424896 | bytes 4526080 | tf_op jit(solution)/shard_map/spcm,pnm->spcn/dot_general | solution.py:91
  87.2 3.6 %add_select_fusion = (f32[16,1024]{1,0:T(8,128)S(1)}, f32[1,1,16,1024]{3,2,0,1:T(8,128)S(1)}) fusion(f32[1,1,16,1024]{3,2,1,0:T(8,128)S(1)} %copy-done.1, f32[1024]{0:T(1024)S(1)} %bitcast.282, pred[]{:T(512)S(6)} %eq.70, f32[16,1024]{1,0:T(8,128)S(1)} %fusion.35, f32[1,1024,1024]{2,1,0:T(8,128)S(1)} %copy-done), kind=kOutput, calls=%fused_computation.40 | convolution fusion | flops 201408512 | bytes 4460545 | tf_op jit(solution)/shard_map/spcm,pnm->spcn/dot_general | solution.py:91
  90.8 28.9 %all-gather.1 = f32[8,17,1024]{2,1,0:T(8,128)S(1)} all-gather(f32[1,17,1024]{2,1,0:T(8,128)S(1)} %maximum_bitcast_fusion.1), channel_id=2, replica_groups=mesh['tm'=8,'sub'=32] {'tm'}, dimensions={0}, use_global_device_ids=true | all-gather | bytes 626688 | tf_op jit(solution)/shard_map/all_gather | solution.py:36
  119.8 0.1 while.12
  119.9 0.6 fusion.41
  (34 shorter events, 0.3 us)
Async XLA Ops:
  4.2 9.2 %copy-start.5 = (s32[1,8]{1,0:T(1,128)S(1)}, s32[1,8]{1,0:T(1,128)}, u32[]{:S(2)}) copy-start(s32[1,8]{1,0:T(1,128)} %param.23) | copy-start | bytes 100
  4.2 17.4 %copy-start.6 = (s32[1,8]{1,0:T(1,128)S(1)}, s32[1,8]{1,0:T(1,128)}, u32[]{:S(2)}) copy-start(s32[1,8]{1,0:T(1,128)} %param.20) | copy-start | bytes 100
  4.2 17.4 %copy-start.7 = (s32[1,8]{1,0:T(1,128)S(1)}, s32[1,8]{1,0:T(1,128)}, u32[]{:S(2)}) copy-start(s32[1,8]{1,0:T(1,128)} %param.21) | copy-start | bytes 100
  4.3 17.4 %copy-start.8 = (f32[1,8]{1,0:T(1,128)S(1)}, f32[1,8]{1,0:T(1,128)}, u32[]{:S(2)}) copy-start(f32[1,8]{1,0:T(1,128)} %param.19) | copy-start | bytes 100
  4.3 17.4 %copy-start.9 = (s32[1,8]{1,0:T(1,128)S(1)}, s32[1,8]{1,0:T(1,128)}, u32[]{:S(2)}) copy-start(s32[1,8]{1,0:T(1,128)} %param.22) | copy-start | bytes 100
  4.3 28.1 %copy-start.1 = (f32[1,1,16,1024]{3,2,1,0:T(8,128)S(1)}, f32[1,1,16,1024]{3,2,1,0:T(8,128)}, u32[]{:S(2)}) copy-start(f32[1,1,16,1024]{3,2,1,0:T(8,128)} %param.14) | copy-start | bytes 196612
  4.3 28.0 %copy-start.2 = (f32[1,16,1024]{2,1,0:T(8,128)S(1)}, f32[1,16,1024]{2,1,0:T(8,128)}, u32[]{:S(2)}) copy-start(f32[1,16,1024]{2,1,0:T(8,128)} %param.17) | copy-start | bytes 196612
  4.3 28.0 %copy-start.4 = (f32[1,1024]{1,0:T(1,128)S(1)}, f32[1,1024]{1,0:T(1,128)}, u32[]{:S(2)}) copy-start(f32[1,1024]{1,0:T(1,128)} %param.16) | copy-start | bytes 12292
  14.3 15.1 %all-to-all-start = ((f32[32,8,1,1,128]{4,1,3,2,0:T(8,128)}), f32[32,8,1,1,128]{4,1,3,2,0:T(8,128)S(1)}, u32[]{:S(2)}, u32[]{:S(2)}) async-start(f32[32,8,1,1,128]{4,1,3,2,0:T(8,128)} %broadcast_in_dim.24), calls=%async_computation | async-start | bytes 262144 | tf_op jit(solution)/shard_map/all_to_all | solution.py:19
  55.3 14.2 %copy-start.3 = (f32[1,1024]{1,0:T(1,128)S(1)}, f32[1,1024]{1,0:T(1,128)}, u32[]{:S(2)}) copy-start(f32[1,1024]{1,0:T(1,128)} %param.18) | copy-start | bytes 12292
  65.4 12.8 %all-to-all-start.1 = ((f32[32,8,2,1,128]{4,1,2,3,0:T(8,128)}), f32[32,8,2,1,128]{4,1,2,3,0:T(8,128)S(1)}, u32[]{:S(2)}, u32[]{:S(2)}) async-start(f32[32,8,2,1,128]{4,1,2,3,0:T(8,128)} %broadcast_in_dim.26), calls=%async_computation.1 | async-start | bytes 524288 | tf_op jit(solution)/shard_map/all_to_all | solution.py:19
  81.3 5.9 %copy-start = (f32[1,1024,1024]{2,1,0:T(8,128)S(1)}, f32[1,1024,1024]{2,1,0:T(8,128)}, u32[]{:S(2)}) copy-start(f32[1,1024,1024]{2,1,0:T(8,128)} %param.15) | copy-start | bytes 12582916
where the time goes:
time: 121 us
  local copies, waits for them, and re-layouts  38.2 us (32%)
  blocking collectives  28.9 us (24%)
  matrix products  21.9 us (18%)
  waiting for transfers between devices  16.4 us (14%)
  starting transfers between devices  11.4 us (9%)
  other arithmetic  3.1 us (3%)
    all_gather x1, blocking collectives, all_in_one(): both, at, found = (lax.all_gather(jnp.concatenate(lines), axis), 0, {})  28.9 us
    gather x7, local copies, waits for them, and re-layouts, terminals(): jnp.take_along_axis(grouped, jnp.broadcast_to(term_block[None, :, None, :...  27.3 us
    dot_general x4, matrix products, advance(): jnp.einsum('spcm,pnm->spcn', driven, inverses, precision=lax.Precision.HI...  20.8 us
    all_to_all x2, waiting for transfers between devices, sent_to_all(): lax.all_to_all(jnp.broadcast_to(shard[None], (count, *shard.shape)), axis...  16.4 us
    all_to_all x2, starting transfers between devices, sent_to_all(): lax.all_to_all(jnp.broadcast_to(shard[None], (count, *shard.shape)), axis...  11.4 us
    reshape x3, local copies, waits for them, and re-layouts, terminals(): state.reshape(state.shape[0], state.shape[1], state.shape[2], state.shape...  3.06 us
  transfers between devices with their start and end apart: 2, of which 2 were waited for; matrix products, arithmetic and copies ran while one was open for 0% of the time, Pallas kernels for 0%

commit v1 on v0

v1 whole, which is shorter than its diff:
```python
import functools

import jax
import jax.numpy as jnp
from jax import lax
from jax.experimental import pallas as pl
from jax.experimental.pallas import tpu as pltpu
from jax.sharding import PartitionSpec as P

TERM = 8
LINES = 8
COLS = 16
LANES = 128
NODES = 1024
CHUNKS = 8
MESH = pl.DeviceIdType.MESH
F32 = jnp.float32
BF16 = jnp.bfloat16


def split(x):
    high = x.astype(BF16)
    low = (x - high.astype(F32)).astype(BF16)
    return high, low


def dot(a, b):
    return jnp.dot(a, b, preferred_element_type=F32)


def packed(ref, at, offset):
    group = lax.broadcasted_iota(jnp.int32, (LINES, LANES), 1) // COLS
    out = jnp.zeros((LINES, LANES), F32)
    for t in range(TERM):
        rows = ref[at, pl.ds(t, LINES, stride=TERM), :]
        shift = (COLS * t - offset) % LANES
        rows = pltpu.roll(rows, shift, 1) if shift else rows
        out = jnp.where(group == t, rows, out)
    return out


def unpacked(far):
    return jnp.concatenate(
        [far] + [pltpu.roll(far, LANES - COLS * t, 1) for t in range(1, TERM)], axis=0
    )


def kernel(
    slices, subs,
    starts_h, inverses_h, retain_h, sources_h, decay_h,
    admittance, partner, delay, live, block,
    out_ref,
    starts, sources, retain, decay,
    raw, a_high, a_low, z_all, z_turned, z_both, m_high, m_low,
    rows, near0, near12, ends_in, far0, far1,
    in_sems, raw_sems, send_sems, recv0, recv12, z_send, z_recv,
):
    zed = lax.axis_index("tm")
    me = lax.axis_index("sub")

    far0[...] = jnp.zeros_like(far0)
    far1[...] = jnp.zeros_like(far1)

    barrier = pltpu.get_barrier_semaphore()

    @pl.loop(1, subs)
    def _(o):
        pl.semaphore_signal(
            barrier, inc=1, device_id={"sub": lax.rem(me + o, subs)}, device_id_type=MESH
        )

    @pl.loop(1, slices)
    def _(o):
        pl.semaphore_signal(
            barrier, inc=1, device_id={"tm": lax.rem(zed + o, slices)}, device_id_type=MESH
        )

    pairs = (
        (starts_h, starts), (retain_h, retain), (sources_h, sources), (decay_h, decay),
    )
    loads = [pltpu.make_async_copy(a, b, in_sems.at[k]) for k, (a, b) in enumerate(pairs)]
    depth = NODES // CHUNKS
    chunks = [
        pltpu.make_async_copy(
            inverses_h.at[pl.ds(k * depth, depth), :], raw.at[pl.ds(k * depth, depth), :],
            raw_sems.at[k],
        )
        for k in range(CHUNKS)
    ]
    for load in loads:
        load.start()
    for chunk in chunks:
        chunk.start()
    for load in loads:
        load.wait()

    gain = retain[...]
    inverse_gain = 1.0 / gain
    lane = lax.broadcasted_iota(jnp.int32, (LINES, NODES), 1)
    slot = lax.broadcasted_iota(jnp.int32, (LINES, NODES), 0)
    first = jnp.zeros((LINES, NODES), jnp.int32)
    for l in range(LINES):
        first = jnp.where(slot == l, block[0, l] * TERM, first)
    ones = [(lane == first + t).astype(F32) for t in range(TERM)]
    inputs = jnp.concatenate(
        [
            starts[...],
            sources[...] * inverse_gain,
            jnp.zeros((COLS, NODES), F32),
            jnp.broadcast_to(inverse_gain, (COLS, NODES)),
        ]
        + ones,
        axis=0,
    )
    turned = jnp.transpose(inputs)
    z_all[0] = turned.reshape(NODES // TERM, TERM, LANES)

    def pick(at):
        for l in range(LINES):
            rows[at, pl.ds(l * TERM, TERM), :] = z_all[at, block[0, l]]

    pick(0)
    near0[me] = packed(rows, 0, 0)

    pl.semaphore_wait(barrier, subs - 1 + slices - 1)

    def sub_copy(ref, send, recv, o):
        return pltpu.make_async_remote_copy(
            src_ref=ref.at[me], dst_ref=ref.at[me], send_sem=send, recv_sem=recv,
            device_id={"sub": lax.rem(me + o, subs)}, device_id_type=MESH,
        )

    def all_of(ref, send, recv):
        whole = ref.at[pl.ds(0, subs - 1)]
        return pltpu.make_async_remote_copy(
            src_ref=whole, dst_ref=whole, send_sem=send, recv_sem=recv,
            device_id={"sub": lax.rem(me + 1, subs)}, device_id_type=MESH,
        )

    @pl.loop(1, subs)
    def _(o):
        sub_copy(near0, send_sems.at[0], recv0, o).start()

    slot8 = lax.broadcasted_iota(jnp.int32, (LINES, LANES), 0)
    weight = jnp.zeros((LINES, LANES), F32)
    for l in range(LINES):
        weight = jnp.where(slot8 == l, admittance[0, l] * live[0, l].astype(F32), weight)
    weight = weight * packed(rows, 0, 3 * COLS)

    high, low = split(turned)
    z_both[:, :LANES] = high
    z_both[:, LANES:] = low
    for k in range(CHUNKS):
        chunks[k].wait()
        piece = pl.ds(k * depth, depth)
        high, low = split(raw[piece, :] * gain)
        a_high[piece, :] = high
        a_low[piece, :] = low

    @pl.loop(1, 5)
    def _(k):
        both = z_both[...]
        y = dot(a_high[...], both) + dot(a_low[...], both)
        new = y[:, :LANES] + y[:, LANES:]
        z_all[k] = new.reshape(NODES // TERM, TERM, LANES)
        high, low = split(new)
        z_both[:, :LANES] = high
        z_both[:, LANES:] = low
        z_turned[k - 1] = jnp.transpose(new)

    mine_z = pl.ds(pl.multiple_of(zed * COLS, COLS), COLS)
    base = z_turned[3, :COLS, :]
    for k in range(4):
        base = base + z_turned[k, COLS : 2 * COLS, :]
    slope = decay[...]
    base = jnp.where(zed == 0, base, base - slope * starts[...])
    ends_in[mine_z, :] = base

    def z_copy(ref, which, d):
        return pltpu.make_async_remote_copy(
            src_ref=ref.at[mine_z, :], dst_ref=ref.at[mine_z, :],
            send_sem=z_send.at[which, d], recv_sem=z_recv.at[which, d],
            device_id={"tm": lax.rem(zed + d, slices)}, device_id_type=MESH,
        )

    def z_start(ref, which):
        @pl.loop(1, slices)
        def _(d):
            @pl.when(zed + d < slices)
            def _():
                z_copy(ref, which, d).start()

    def z_arrive(ref, which):
        @pl.loop(1, slices)
        def _(d):
            @pl.when(zed >= d)
            def _():
                z_copy(ref, which, d).wait_recv()

    def z_sent(ref, which):
        @pl.loop(1, slices)
        def _(d):
            @pl.when(zed + d < slices)
            def _():
                z_copy(ref, which, d).wait_send()

    z_start(ends_in, 0)

    pick(1)
    pick(2)
    lanes64 = lax.broadcasted_iota(jnp.int32, (LINES * TERM, LANES), 1)
    first_rows = rows[1]
    second_rows = rows[2] + jnp.where(lanes64 >= COLS, first_rows, 0.0)
    q_high, q_low = split(jnp.concatenate([first_rows, second_rows], axis=0))
    q_both = jnp.concatenate([q_high, q_low], axis=1)
    r32 = lax.broadcasted_iota(jnp.int32, (4 * COLS, LANES), 0)
    c32 = lax.broadcasted_iota(jnp.int32, (4 * COLS, LANES), 1)
    unit = jnp.where(
        (c32 < COLS) & (r32 < 2 * COLS) & ((r32 == c32) | (r32 == c32 + COLS)), 1.0, 0.0
    ).astype(F32)

    all_of(near0, send_sems.at[0], recv0).wait_recv()
    def row_of(tile, l):
        return jnp.sum(jnp.where(slot8 == lax.rem(partner[0, l], LINES), tile, 0.0), axis=0, keepdims=True)

    olds = jnp.zeros((LINES, LANES), F32)
    for l in range(LINES):
        olds = jnp.where(slot8 == l, row_of(near0[lax.div(partner[0, l], LINES)], l), olds)
    spread0 = unpacked(olds * weight)
    e_high, e_low = split(jnp.concatenate([unit, spread0], axis=0))
    e_both = jnp.concatenate([e_high, e_low], axis=1)
    e_both = jnp.concatenate([e_both, e_both], axis=0)
    s = dot(q_both, e_both)
    s = s[:, :LANES] + s[:, LANES:]
    rows[1] = s[: LINES * TERM]
    rows[2] = s[LINES * TERM :]
    near12[me, 0] = packed(rows, 1, 0)
    near12[me, 1] = packed(rows, 2, 0)

    @pl.loop(1, subs)
    def _(o):
        sub_copy(near12, send_sems.at[1], recv12, o).start()

    blank = jnp.zeros((LINES * TERM, LANES), F32)
    far0[mine_z, :] = jnp.transpose(jnp.concatenate([spread0, blank], axis=0))[:COLS]
    z_start(far0, 1)

    half = LINES * TERM
    effect = jnp.concatenate(
        [
            z_turned[2, half:, :] + z_turned[3, half:, :],
            jnp.zeros((half, NODES), F32),
            z_turned[1, half:, :],
            z_turned[0, half:, :],
        ],
        axis=0,
    )
    high, low = split(effect)
    m_high[...] = high
    m_low[...] = low

    all_of(near12, send_sems.at[1], recv12).wait_recv()
    fars = []
    for step in (2, 3):
        far = olds
        for l in range(LINES):
            reach = step + 1 - delay[0, l]
            late = jnp.minimum(jnp.maximum(reach, 1), 2) - 1
            row = row_of(near12[lax.div(partner[0, l], LINES), late], l)
            far = jnp.where((slot8 == l) & (jnp.full((LINES, LANES), reach, jnp.int32) > 0), row, far)
        fars.append(unpacked(far * weight))
    spread = jnp.concatenate(fars, axis=0)
    far1[mine_z, :] = jnp.transpose(spread)[:COLS]
    z_start(far1, 2)

    z_arrive(ends_in, 0)

    def one(i, state):
        return slope * state + ends_in[pl.ds(pl.multiple_of(i * COLS, COLS), COLS), :]

    plain = lax.fori_loop(0, zed + 1, one, jnp.zeros((COLS, NODES), F32))

    z_arrive(far0, 1)
    z_arrive(far1, 2)
    high, low = split(jnp.concatenate([far0[...], far1[...]], axis=1))
    count = slices * COLS
    y = dot(jnp.concatenate([high, low], axis=0), m_high[...])
    y = y[:count] + y[count:] + dot(high, m_low[...])
    state = jnp.zeros((COLS, NODES), F32)
    for i in range(slices):
        state = jnp.where(i <= zed, slope * state + y[i * COLS : (i + 1) * COLS], state)
    out_ref[...] = plain + state

    all_of(near0, send_sems.at[0], recv0).wait_send()
    all_of(near12, send_sems.at[1], recv12).wait_send()
    z_sent(ends_in, 0)
    z_sent(far0, 1)
    z_sent(far1, 2)


def shards(slices, subs, starts, inverses, retain, sources, decay, admittance, partner, delay, live, block):
    vmem, smem = pltpu.VMEM, pltpu.SMEM
    out = pl.pallas_call(
        functools.partial(kernel, slices, subs),
        out_shape=jax.ShapeDtypeStruct((COLS, NODES), F32),
        in_specs=[pl.BlockSpec(memory_space=pltpu.HBM)] * 5 + [pl.BlockSpec(memory_space=smem)] * 5,
        out_specs=pl.BlockSpec(memory_space=pltpu.VMEM),
        scratch_shapes=[
            vmem((COLS, NODES), F32), vmem((COLS, NODES), F32),
            vmem((1, NODES), F32), vmem((1, NODES), F32),
            vmem((NODES, NODES), F32), vmem((NODES, NODES), BF16), vmem((NODES, NODES), BF16),
            vmem((5, NODES // TERM, TERM, LANES), F32), vmem((4, LANES, NODES), F32),
            vmem((NODES, 2 * LANES), BF16),
            vmem((2 * LANES, NODES), BF16), vmem((2 * LANES, NODES), BF16),
            vmem((3, LINES * TERM, LANES), F32),
            vmem((subs, LINES, LANES), F32), vmem((subs, 2, LINES, LANES), F32),
            vmem((slices * COLS, NODES), F32),
            vmem((slices * COLS, LANES), F32), vmem((slices * COLS, LANES), F32),
            pltpu.SemaphoreType.DMA((4,)), pltpu.SemaphoreType.DMA((CHUNKS,)),
            pltpu.SemaphoreType.DMA((2,)), pltpu.SemaphoreType.DMA, pltpu.SemaphoreType.DMA,
            pltpu.SemaphoreType.DMA((3, slices)), pltpu.SemaphoreType.DMA((3, slices)),
        ],
        compiler_params=pltpu.CompilerParams(
            collective_id=0, has_side_effects=True, vmem_limit_bytes=48 * 1024 * 1024
        ),
    )(
        starts.reshape(COLS, NODES), inverses.reshape(NODES, NODES), retain,
        sources.reshape(COLS, NODES), decay, admittance, partner, delay, live, block,
    )
    return out.reshape(1, 1, COLS, NODES)


def solution(mesh):
    return jax.shard_map(
        functools.partial(shards, mesh.shape["tm"], mesh.shape["sub"]),
        mesh=mesh,
        in_specs=(
            P("tm", "sub", None, None),
            P("sub", None, None),
            P("sub", None),
            P("sub", None, None),
            P("sub", None),
            P("sub", None),
            P("sub", None),
            P("sub", None),
            P("sub", None),
            P("sub", None),
        ),
        out_specs=P("tm", "sub", None, None),
        check_vma=False,
    )
```

time: 121 us -> 39.4 us (0.33)
  the two profiles are of different devices: /device:TPU:32 before, /device:TPU:192 now
where the time goes in v1:
time: 39.4 us; the launch traced here: 39.1 us
  Pallas kernels  29.9 us (76%)
  local copies, waits for them, and re-layouts  9.14 us (23%)
    pallas_call x1, Pallas kernels, shards(): pl.pallas_call(functools.partial(kernel, slices, subs), out_shape=jax.Sha...  29.9 us
    unnamed x21, local copies, waits for them, and re-layouts  9.14 us

profile of v1, /device:TPU:192, one launch (start us, length us, event | category | flops | bytes accessed | tf_op | source)
XLA Modules:
  0.0 39.1 jit_solution(3373822956152181263)
XLA Ops:
  0.0 0.0 copy-start
  0.0 2.2 %copy-done = f32[1,1024,1024]{2,1,0:T(8,128)S(1)} copy-done((f32[1,1024,1024]{2,1,0:T(8,128)S(1)}, f32[1,1024,1024]{2,1,0:T(8,128)}, u32[]{:S(2)}) %copy-start) | copy-done | bytes 4194328
  2.2 0.0 copy-start.1
  2.2 0.8 %copy-done.1 = f32[1,1,16,1024]{3,2,1,0:T(8,128)S(1)} copy-done((f32[1,1,16,1024]{3,2,1,0:T(8,128)S(1)}, f32[1,1,16,1024]{3,2,1,0:T(8,128)}, u32[]{:S(2)}) %copy-start.1) | copy-done | bytes 65560
  3.0 0.0 copy-start.2
  3.0 0.8 %copy-done.2 = f32[1,16,1024]{2,1,0:T(8,128)S(1)} copy-done((f32[1,16,1024]{2,1,0:T(8,128)S(1)}, f32[1,16,1024]{2,1,0:T(8,128)}, u32[]{:S(2)}) %copy-start.2) | copy-done | bytes 65560
  3.9 0.0 copy-start.3
  3.9 0.7 %copy-done.3 = f32[1,1024]{1,0:T(1,128)S(1)} copy-done((f32[1,1024]{1,0:T(1,128)S(1)}, f32[1,1024]{1,0:T(1,128)}, u32[]{:S(2)}) %copy-start.3) | copy-done | bytes 4120
  4.6 0.0 copy-start.4
  4.6 0.7 %copy-done.4 = f32[1,1024]{1,0:T(1,128)S(1)} copy-done((f32[1,1024]{1,0:T(1,128)S(1)}, f32[1,1024]{1,0:T(1,128)}, u32[]{:S(2)}) %copy-start.4) | copy-done | bytes 4120
  5.2 0.0 copy-start.5
  5.2 0.7 %copy-done.5 = f32[1,8]{1,0:T(1,128)S(1)} copy-done((f32[1,8]{1,0:T(1,128)S(1)}, f32[1,8]{1,0:T(1,128)}, u32[]{:S(2)}) %copy-start.5) | copy-done | bytes 56
  5.9 0.0 copy-start.6
  5.9 0.7 %copy-done.6 = s32[1,8]{1,0:T(1,128)S(1)} copy-done((s32[1,8]{1,0:T(1,128)S(1)}, s32[1,8]{1,0:T(1,128)}, u32[]{:S(2)}) %copy-start.6) | copy-done | bytes 56
  6.6 0.0 copy-start.7
  6.6 0.7 %copy-done.7 = s32[1,8]{1,0:T(1,128)S(1)} copy-done((s32[1,8]{1,0:T(1,128)S(1)}, s32[1,8]{1,0:T(1,128)}, u32[]{:S(2)}) %copy-start.7) | copy-done | bytes 56
  7.2 0.0 copy-start.8
  7.2 0.7 %copy-done.8 = s32[1,8]{1,0:T(1,128)S(1)} copy-done((s32[1,8]{1,0:T(1,128)S(1)}, s32[1,8]{1,0:T(1,128)}, u32[]{:S(2)}) %copy-start.8) | copy-done | bytes 56
  7.9 0.0 copy-start.9
  7.9 0.7 %copy-done.9 = s32[1,8]{1,0:T(1,128)S(1)} copy-done((s32[1,8]{1,0:T(1,128)S(1)}, s32[1,8]{1,0:T(1,128)}, u32[]{:S(2)}) %copy-start.9) | copy-done | bytes 56
  8.5 29.9 %shard_map.100 = f32[16,1024]{1,0:T(8,128)S(1)} custom-call(f32[16,1024]{1,0:T(8,128)S(1)} %bitcast.6, f32[1024,1024]{1,0:T(8,128)S(1)} %bitcast.4, f32[1,1024]{1,0:T(1,128)S(1)} %copy-done.3, f32[16,1024]{1,0:T(8,128)S(1)} %bitcast.7, f32[1,1024]{1,0:T(1,128)S(1)} %copy-done.4, f32[1,8]{1,0:T(1,128)S(1)} %copy-done.5, s32[1,8]{1,0:T(1,128)S(1)} %copy-done.6, ...), custom_call_target="tpu_custom_call" | custom-call | tf_op jit(solution)/shard_map/pallas_call | solution.py:303
  38.5 0.6 %copy.12 = f32[1,1,16,1024]{3,2,1,0:T(8,128)} copy(f32[1,1,16,1024]{3,2,1,0:T(8,128)S(1)} %bitcast.5) | data formatting | bytes 131072
Async XLA Ops:
  0.0 2.2 %copy-start = (f32[1,1024,1024]{2,1,0:T(8,128)S(1)}, f32[1,1024,1024]{2,1,0:T(8,128)}, u32[]{:S(2)}) copy-start(f32[1,1024,1024]{2,1,0:T(8,128)} %param.11) | copy-start | bytes 12582916
  2.2 0.8 %copy-start.1 = (f32[1,1,16,1024]{3,2,1,0:T(8,128)S(1)}, f32[1,1,16,1024]{3,2,1,0:T(8,128)}, u32[]{:S(2)}) copy-start(f32[1,1,16,1024]{3,2,1,0:T(8,128)} %param.10) | copy-start | bytes 196612
  3.0 0.8 %copy-start.2 = (f32[1,16,1024]{2,1,0:T(8,128)S(1)}, f32[1,16,1024]{2,1,0:T(8,128)}, u32[]{:S(2)}) copy-start(f32[1,16,1024]{2,1,0:T(8,128)} %param.13) | copy-start | bytes 196612
  3.9 0.7 %copy-start.3 = (f32[1,1024]{1,0:T(1,128)S(1)}, f32[1,1024]{1,0:T(1,128)}, u32[]{:S(2)}) copy-start(f32[1,1024]{1,0:T(1,128)} %retain_h.1) | copy-start | bytes 12292
  4.6 0.7 %copy-start.4 = (f32[1,1024]{1,0:T(1,128)S(1)}, f32[1,1024]{1,0:T(1,128)}, u32[]{:S(2)}) copy-start(f32[1,1024]{1,0:T(1,128)} %decay_h.1) | copy-start | bytes 12292
  5.2 0.7 %copy-start.5 = (f32[1,8]{1,0:T(1,128)S(1)}, f32[1,8]{1,0:T(1,128)}, u32[]{:S(2)}) copy-start(f32[1,8]{1,0:T(1,128)} %admittance.1) | copy-start | bytes 100
  5.9 0.7 %copy-start.6 = (s32[1,8]{1,0:T(1,128)S(1)}, s32[1,8]{1,0:T(1,128)}, u32[]{:S(2)}) copy-start(s32[1,8]{1,0:T(1,128)} %partner.1) | copy-start | bytes 100
  6.6 0.7 %copy-start.7 = (s32[1,8]{1,0:T(1,128)S(1)}, s32[1,8]{1,0:T(1,128)}, u32[]{:S(2)}) copy-start(s32[1,8]{1,0:T(1,128)} %delay.1) | copy-start | bytes 100
  7.2 0.7 %copy-start.8 = (s32[1,8]{1,0:T(1,128)S(1)}, s32[1,8]{1,0:T(1,128)}, u32[]{:S(2)}) copy-start(s32[1,8]{1,0:T(1,128)} %live.1) | copy-start | bytes 100
  7.9 0.7 %copy-start.9 = (s32[1,8]{1,0:T(1,128)S(1)}, s32[1,8]{1,0:T(1,128)}, u32[]{:S(2)}) copy-start(s32[1,8]{1,0:T(1,128)} %block.1) | copy-start | bytes 100

commit v2 on v1

--- a/solution.py
+++ b/solution.py
@@ -48,9 +48,9 @@
 def kernel(
     slices, subs,
     starts_h, inverses_h, retain_h, sources_h, decay_h,
-    admittance, partner, delay, live, block,
+    admittance_h, partner_h, delay_h, live_h, block_h,
     out_ref,
-    starts, sources, retain, decay,
+    starts, sources, retain, decay, admittance, partner, delay, live, block,
     raw, a_high, a_low, z_all, z_turned, z_both, m_high, m_low,
     rows, near0, near12, ends_in, far0, far1,
     in_sems, raw_sems, send_sems, recv0, recv12, z_send, z_recv,
@@ -76,7 +76,9 @@
         )
 
     pairs = (
-        (starts_h, starts), (retain_h, retain), (sources_h, sources), (decay_h, decay),
+        (starts_h, starts), (block_h, block), (retain_h, retain), (sources_h, sources),
+        (partner_h, partner), (admittance_h, admittance), (live_h, live), (delay_h, delay),
+        (decay_h, decay),
     )
     loads = [pltpu.make_async_copy(a, b, in_sems.at[k]) for k, (a, b) in enumerate(pairs)]
     depth = NODES // CHUNKS
@@ -303,11 +305,13 @@
     out = pl.pallas_call(
         functools.partial(kernel, slices, subs),
         out_shape=jax.ShapeDtypeStruct((COLS, NODES), F32),
-        in_specs=[pl.BlockSpec(memory_space=pltpu.HBM)] * 5 + [pl.BlockSpec(memory_space=smem)] * 5,
+        in_specs=[pl.BlockSpec(memory_space=pltpu.HBM)] * 10,
         out_specs=pl.BlockSpec(memory_space=pltpu.VMEM),
         scratch_shapes=[
             vmem((COLS, NODES), F32), vmem((COLS, NODES), F32),
             vmem((1, NODES), F32), vmem((1, NODES), F32),
+            smem((1, LINES), F32), smem((1, LINES), jnp.int32), smem((1, LINES), jnp.int32),
+            smem((1, LINES), jnp.int32), smem((1, LINES), jnp.int32),
             vmem((NODES, NODES), F32), vmem((NODES, NODES), BF16), vmem((NODES, NODES), BF16),
             vmem((5, NODES // TERM, TERM, LANES), F32), vmem((4, LANES, NODES), F32),
             vmem((NODES, 2 * LANES), BF16),
@@ -316,12 +320,12 @@
             vmem((subs, LINES, LANES), F32), vmem((subs, 2, LINES, LANES), F32),
             vmem((slices * COLS, NODES), F32),
             vmem((slices * COLS, LANES), F32), vmem((slices * COLS, LANES), F32),
-            pltpu.SemaphoreType.DMA((4,)), pltpu.SemaphoreType.DMA((CHUNKS,)),
+            pltpu.SemaphoreType.DMA((9,)), pltpu.SemaphoreType.DMA((CHUNKS,)),
             pltpu.SemaphoreType.DMA((2,)), pltpu.SemaphoreType.DMA, pltpu.SemaphoreType.DMA,
             pltpu.SemaphoreType.DMA((3, slices)), pltpu.SemaphoreType.DMA((3, slices)),
         ],
         compiler_params=pltpu.CompilerParams(
-            collective_id=0, has_side_effects=True, vmem_limit_bytes=48 * 1024 * 1024
+            collective_id=0, has_side_effects=True, vmem_limit_bytes=67043328
         ),
     )(
         starts.reshape(COLS, NODES), inverses.reshape(NODES, NODES), retain,

time: 39.4 us -> 31.6 us (0.80)
  local copies, waits for them, and re-layouts: 9.14 us -> 1.47 us
    unnamed x21 -> x1, local copies, waits for them, and re-layouts: 9.14 us -> 1.47 us
where the time goes in v2:
time: 31.6 us; the launch traced here: 31.4 us
  Pallas kernels  30 us (95%)
  local copies, waits for them, and re-layouts  1.47 us (5%)
    pallas_call x1, Pallas kernels, shards(): pl.pallas_call(functools.partial(kernel, slices, subs), out_shape=jax.Sha...  30 us
    unnamed x1, local copies, waits for them, and re-layouts  1.47 us

profile of v2, /device:TPU:192, one launch (start us, length us, event | category | flops | bytes accessed | tf_op | source)
XLA Modules:
  0.0 31.4 jit_solution(9499290371115069028)
XLA Ops:
  0.0 30.0 %shard_map.100 = f32[16,1024]{1,0:T(8,128)} custom-call(f32[16,1024]{1,0:T(8,128)} %bitcast.6, f32[1024,1024]{1,0:T(8,128)} %bitcast.4, f32[1,1024]{1,0:T(1,128)} %retain_h.1, f32[16,1024]{1,0:T(8,128)} %bitcast.7, f32[1,1024]{1,0:T(1,128)} %decay_h.1, f32[1,8]{1,0:T(1,128)} %admittance_h.1, s32[1,8]{1,0:T(1,128)} %partner_h.1, s32[1,8]{1,0:T(1,128)} %delay_h.1, ...), custom_call_target="tpu_custom_call" | custom-call | tf_op jit(solution)/shard_map/pallas_call | solution.py:305
  30.0 1.5 %copy.12 = f32[1,1,16,1024]{3,2,1,0:T(8,128)} copy(f32[1,1,16,1024]{3,2,1,0:T(8,128)} %bitcast.5) | data formatting | bytes 131072

commit v3 on v2

--- a/solution.py
+++ b/solution.py
@@ -52,9 +52,11 @@
     out_ref,
     starts, sources, retain, decay, admittance, partner, delay, live, block,
     raw, a_high, a_low, z_all, z_turned, z_both, m_high, m_low,
-    rows, near0, near12, ends_in, far0, far1,
+    rows, near0, near12, offset, parts_in, sums, plain, far0, far1,
     in_sems, raw_sems, send_sems, recv0, recv12, z_send, z_recv,
+    part_send, part_recv, sum_send, sum_recv, ready,
 ):
+    group = slices // 2
     zed = lax.axis_index("tm")
     me = lax.axis_index("sub")
 
@@ -71,9 +73,11 @@
 
     @pl.loop(1, slices)
     def _(o):
-        pl.semaphore_signal(
-            barrier, inc=1, device_id={"tm": lax.rem(zed + o, slices)}, device_id_type=MESH
-        )
+        @pl.when(zed + o < slices)
+        def _():
+            pl.semaphore_signal(
+                barrier, inc=1, device_id={"tm": lax.rem(zed + o, slices)}, device_id_type=MESH
+            )
 
     pairs = (
         (starts_h, starts), (block_h, block), (retain_h, retain), (sources_h, sources),
@@ -124,7 +128,16 @@
     pick(0)
     near0[me] = packed(rows, 0, 0)
 
-    pl.semaphore_wait(barrier, subs - 1 + slices - 1)
+    pl.semaphore_wait(barrier, subs - 1 + zed)
+
+    @pl.loop(1, slices)
+    def _(o):
+        @pl.when(zed >= o)
+        def _():
+            pl.semaphore_signal(
+                ready, inc=1, device_id={"tm": lax.rem(zed + slices - o, slices)},
+                device_id_type=MESH,
+            )
 
     def sub_copy(ref, send, recv, o):
         return pltpu.make_async_remote_copy(
@@ -176,7 +189,36 @@
         base = base + z_turned[k, COLS : 2 * COLS, :]
     slope = decay[...]
     base = jnp.where(zed == 0, base, base - slope * starts[...])
-    ends_in[mine_z, :] = base
+    width = NODES // group
+    for k in range(group):
+        offset[k] = base[:, k * width : (k + 1) * width]
+    side = lax.div(zed, group)
+    place = lax.rem(zed, group)
+    parts_in[zed] = offset[place]
+
+    def part_copy(to, sender):
+        return pltpu.make_async_remote_copy(
+            src_ref=offset.at[lax.rem(to, group)], dst_ref=parts_in.at[zed],
+            send_sem=part_send.at[to], recv_sem=part_recv.at[sender],
+            device_id={"tm": to}, device_id_type=MESH,
+        )
+
+    def sum_copy(to, owner):
+        return pltpu.make_async_remote_copy(
+            src_ref=sums.at[to], dst_ref=plain.at[place],
+            send_sem=sum_send.at[to], recv_sem=sum_recv.at[owner],
+            device_id={"tm": side * group + to}, device_id_type=MESH,
+        )
+
+    @pl.when(zed < slices - 1)
+    def _():
+        pl.semaphore_wait(ready, slices - 1 - zed)
+
+    @pl.loop(0, slices)
+    def _(to):
+        @pl.when((lax.div(to, group) >= side) & (to != zed))
+        def _():
+            part_copy(to, zed).start()
 
     def z_copy(ref, which, d):
         return pltpu.make_async_remote_copy(
@@ -205,8 +247,6 @@
             @pl.when(zed + d < slices)
             def _():
                 z_copy(ref, which, d).wait_send()
-
-    z_start(ends_in, 0)
 
     pick(1)
     pick(2)
@@ -245,7 +285,7 @@
 
     blank = jnp.zeros((LINES * TERM, LANES), F32)
     far0[mine_z, :] = jnp.transpose(jnp.concatenate([spread0, blank], axis=0))[:COLS]
-    z_start(far0, 1)
+    z_start(far0, 0)
 
     half = LINES * TERM
     effect = jnp.concatenate(
@@ -273,17 +313,39 @@
         fars.append(unpacked(far * weight))
     spread = jnp.concatenate(fars, axis=0)
     far1[mine_z, :] = jnp.transpose(spread)[:COLS]
-    z_start(far1, 2)
-
-    z_arrive(ends_in, 0)
+    z_start(far1, 1)
+
+    @pl.loop(0, slices)
+    def _(sender):
+        @pl.when((lax.div(sender, group) <= side) & (sender != zed))
+        def _():
+            part_copy(zed, sender).wait_recv()
+
+    bend = decay[:, pl.ds(pl.multiple_of(place * width, LANES), width)]
 
     def one(i, state):
-        return slope * state + ends_in[pl.ds(pl.multiple_of(i * COLS, COLS), COLS), :]
-
-    plain = lax.fori_loop(0, zed + 1, one, jnp.zeros((COLS, NODES), F32))
-
-    z_arrive(far0, 1)
-    z_arrive(far1, 2)
+        return bend * state + parts_in[i]
+
+    state = lax.fori_loop(0, side * group, one, jnp.zeros((COLS, width), F32))
+    for k in range(group):
+        state = bend * state + parts_in[side * group + k]
+        sums[k] = state
+    plain[place] = sums[place]
+
+    @pl.loop(0, group)
+    def _(to):
+        @pl.when(to != place)
+        def _():
+            sum_copy(to, place).start()
+
+    @pl.loop(0, group)
+    def _(owner):
+        @pl.when(owner != place)
+        def _():
+            sum_copy(owner, owner).wait_recv()
+
+    z_arrive(far0, 0)
+    z_arrive(far1, 1)
     high, low = split(jnp.concatenate([far0[...], far1[...]], axis=1))
     count = slices * COLS
     y = dot(jnp.concatenate([high, low], axis=0), m_high[...])
@@ -291,17 +353,32 @@
     state = jnp.zeros((COLS, NODES), F32)
     for i in range(slices):
         state = jnp.where(i <= zed, slope * state + y[i * COLS : (i + 1) * COLS], state)
-    out_ref[...] = plain + state
+    for k in range(group):
+        part = slice(k * width, (k + 1) * width)
+        out_ref[:, part] = plain[k] + state[:, part]
 
     all_of(near0, send_sems.at[0], recv0).wait_send()
     all_of(near12, send_sems.at[1], recv12).wait_send()
-    z_sent(ends_in, 0)
-    z_sent(far0, 1)
-    z_sent(far1, 2)
+
+    @pl.loop(0, slices)
+    def _(to):
+        @pl.when((lax.div(to, group) >= side) & (to != zed))
+        def _():
+            part_copy(to, zed).wait_send()
+
+    @pl.loop(0, group)
+    def _(to):
+        @pl.when(to != place)
+        def _():
+            sum_copy(to, place).wait_send()
+
+    z_sent(far0, 0)
+    z_sent(far1, 1)
 
 
 def shards(slices, subs, starts, inverses, retain, sources, decay, admittance, partner, delay, live, block):
     vmem, smem = pltpu.VMEM, pltpu.SMEM
+    group = slices // 2
     out = pl.pallas_call(
         functools.partial(kernel, slices, subs),
         out_shape=jax.ShapeDtypeStruct((COLS, NODES), F32),
@@ -318,11 +395,15 @@
             vmem((2 * LANES, NODES), BF16), vmem((2 * LANES, NODES), BF16),
             vmem((3, LINES * TERM, LANES), F32),
             vmem((subs, LINES, LANES), F32), vmem((subs, 2, LINES, LANES), F32),
-            vmem((slices * COLS, NODES), F32),
+            vmem((group, COLS, NODES // group), F32), vmem((slices, COLS, NODES // group), F32),
+            vmem((group, COLS, NODES // group), F32), vmem((group, COLS, NODES // group), F32),
             vmem((slices * COLS, LANES), F32), vmem((slices * COLS, LANES), F32),
             pltpu.SemaphoreType.DMA((9,)), pltpu.SemaphoreType.DMA((CHUNKS,)),
             pltpu.SemaphoreType.DMA((2,)), pltpu.SemaphoreType.DMA, pltpu.SemaphoreType.DMA,
-            pltpu.SemaphoreType.DMA((3, slices)), pltpu.SemaphoreType.DMA((3, slices)),
+            pltpu.SemaphoreType.DMA((2, slices)), pltpu.SemaphoreType.DMA((2, slices)),
+            pltpu.SemaphoreType.DMA((slices,)), pltpu.SemaphoreType.DMA((slices,)),
+            pltpu.SemaphoreType.DMA((group,)), pltpu.SemaphoreType.DMA((group,)),
+            pltpu.SemaphoreType.REGULAR,
         ],
         compiler_params=pltpu.CompilerParams(
             collective_id=0, has_side_effects=True, vmem_limit_bytes=67043328

time: 31.6 us -> 28.4 us (0.90)
  the two profiles are of different devices: /device:TPU:192 before, /device:TPU:1 now
where the time goes in v3:
time: 28.4 us; the launch traced here: 28.3 us
  Pallas kernels  26.8 us (94%)
  local copies, waits for them, and re-layouts  1.47 us (5%)
    pallas_call x1, Pallas kernels, shards(): pl.pallas_call(functools.partial(kernel, slices, subs), out_shape=jax.Sha...  26.8 us
    unnamed x1, local copies, waits for them, and re-layouts  1.47 us

profile of v3, /device:TPU:1, one launch (start us, length us, event | category | flops | bytes accessed | tf_op | source)
XLA Modules:
  0.0 28.3 jit_solution(13101185855193630937)
XLA Ops:
  0.0 26.8 %shard_map.100 = f32[16,1024]{1,0:T(8,128)} custom-call(f32[16,1024]{1,0:T(8,128)} %bitcast.6, f32[1024,1024]{1,0:T(8,128)} %bitcast.4, f32[1,1024]{1,0:T(1,128)} %retain_h.1, f32[16,1024]{1,0:T(8,128)} %bitcast.7, f32[1,1024]{1,0:T(1,128)} %decay_h.1, f32[1,8]{1,0:T(1,128)} %admittance_h.1, s32[1,8]{1,0:T(1,128)} %partner_h.1, s32[1,8]{1,0:T(1,128)} %delay_h.1, ...), custom_call_target="tpu_custom_call" | custom-call | tf_op jit(solution)/shard_map/pallas_call | solution.py:382
  26.8 1.5 %copy.12 = f32[1,1,16,1024]{3,2,1,0:T(8,128)} copy(f32[1,1,16,1024]{3,2,1,0:T(8,128)} %bitcast.5) | data formatting | bytes 131072

commit v4 on v2

--- a/solution.py
+++ b/solution.py
@@ -52,28 +52,17 @@
     out_ref,
     starts, sources, retain, decay, admittance, partner, delay, live, block,
     raw, a_high, a_low, z_all, z_turned, z_both, m_high, m_low,
-    rows, near0, near12, ends_in, far0, far1,
+    rows, near0, near12, offset, parts_in, half_in, prefix, far0, far1,
     in_sems, raw_sems, send_sems, recv0, recv12, z_send, z_recv,
+    part_send, part_recv, half_send, half_recv, prefix_send, prefix_recv, ready,
 ):
+    group = slices // 2
     zed = lax.axis_index("tm")
     me = lax.axis_index("sub")
 
     far0[...] = jnp.zeros_like(far0)
     far1[...] = jnp.zeros_like(far1)
-
-    barrier = pltpu.get_barrier_semaphore()
-
-    @pl.loop(1, subs)
-    def _(o):
-        pl.semaphore_signal(
-            barrier, inc=1, device_id={"sub": lax.rem(me + o, subs)}, device_id_type=MESH
-        )
-
-    @pl.loop(1, slices)
-    def _(o):
-        pl.semaphore_signal(
-            barrier, inc=1, device_id={"tm": lax.rem(zed + o, slices)}, device_id_type=MESH
-        )
+    prefix[...] = jnp.zeros_like(prefix)
 
     pairs = (
         (starts_h, starts), (block_h, block), (retain_h, retain), (sources_h, sources),
@@ -93,6 +82,22 @@
         load.start()
     for chunk in chunks:
         chunk.start()
+    barrier = pltpu.get_barrier_semaphore()
+
+    @pl.loop(1, subs)
+    def _(o):
+        pl.semaphore_signal(
+            barrier, inc=1, device_id={"sub": lax.rem(me + o, subs)}, device_id_type=MESH
+        )
+
+    @pl.loop(1, slices)
+    def _(o):
+        @pl.when(zed + o < slices)
+        def _():
+            pl.semaphore_signal(
+                barrier, inc=1, device_id={"tm": lax.rem(zed + o, slices)}, device_id_type=MESH
+            )
+
     for load in loads:
         load.wait()
 
@@ -124,7 +129,16 @@
     pick(0)
     near0[me] = packed(rows, 0, 0)
 
-    pl.semaphore_wait(barrier, subs - 1 + slices - 1)
+    pl.semaphore_wait(barrier, subs - 1 + zed)
+
+    @pl.loop(1, slices)
+    def _(o):
+        @pl.when(zed >= o)
+        def _():
+            pl.semaphore_signal(
+                ready.at[zed], inc=1, device_id={"tm": lax.rem(zed + slices - o, slices)},
+                device_id_type=MESH,
+            )
 
     def sub_copy(ref, send, recv, o):
         return pltpu.make_async_remote_copy(
@@ -159,8 +173,7 @@
         a_high[piece, :] = high
         a_low[piece, :] = low
 
-    @pl.loop(1, 5)
-    def _(k):
+    def advance(k):
         both = z_both[...]
         y = dot(a_high[...], both) + dot(a_low[...], both)
         new = y[:, :LANES] + y[:, LANES:]
@@ -170,43 +183,9 @@
         z_both[:, LANES:] = low
         z_turned[k - 1] = jnp.transpose(new)
 
-    mine_z = pl.ds(pl.multiple_of(zed * COLS, COLS), COLS)
-    base = z_turned[3, :COLS, :]
-    for k in range(4):
-        base = base + z_turned[k, COLS : 2 * COLS, :]
-    slope = decay[...]
-    base = jnp.where(zed == 0, base, base - slope * starts[...])
-    ends_in[mine_z, :] = base
-
-    def z_copy(ref, which, d):
-        return pltpu.make_async_remote_copy(
-            src_ref=ref.at[mine_z, :], dst_ref=ref.at[mine_z, :],
-            send_sem=z_send.at[which, d], recv_sem=z_recv.at[which, d],
-            device_id={"tm": lax.rem(zed + d, slices)}, device_id_type=MESH,
-        )
-
-    def z_start(ref, which):
-        @pl.loop(1, slices)
-        def _(d):
-            @pl.when(zed + d < slices)
-            def _():
-                z_copy(ref, which, d).start()
-
-    def z_arrive(ref, which):
-        @pl.loop(1, slices)
-        def _(d):
-            @pl.when(zed >= d)
-            def _():
-                z_copy(ref, which, d).wait_recv()
-
-    def z_sent(ref, which):
-        @pl.loop(1, slices)
-        def _(d):
-            @pl.when(zed + d < slices)
-            def _():
-                z_copy(ref, which, d).wait_send()
-
-    z_start(ends_in, 0)
+    @pl.loop(1, 4)
+    def _(k):
+        advance(k)
 
     pick(1)
     pick(2)
@@ -243,9 +222,87 @@
     def _(o):
         sub_copy(near12, send_sems.at[1], recv12, o).start()
 
+    advance(4)
+
+    mine_z = pl.ds(pl.multiple_of(zed * COLS, COLS), COLS)
+    base = z_turned[3, :COLS, :]
+    for k in range(4):
+        base = base + z_turned[k, COLS : 2 * COLS, :]
+    slope = decay[...]
+    base = jnp.where(zed == 0, base, base - slope * starts[...])
+    width = NODES // group
+    for k in range(group):
+        offset[k] = base[:, k * width : (k + 1) * width]
+    side = lax.div(zed, group)
+    place = lax.rem(zed, group)
+    half_in[place] = offset[...]
+
+    def half_copy(to, sender):
+        return pltpu.make_async_remote_copy(
+            src_ref=offset, dst_ref=half_in.at[place],
+            send_sem=half_send.at[to], recv_sem=half_recv.at[sender],
+            device_id={"tm": side * group + to}, device_id_type=MESH,
+        )
+
+    def part_copy(to, sender):
+        return pltpu.make_async_remote_copy(
+            src_ref=offset.at[to], dst_ref=parts_in.at[place],
+            send_sem=part_send.at[to], recv_sem=part_recv.at[sender],
+            device_id={"tm": group + to}, device_id_type=MESH,
+        )
+
+    def prefix_copy(to, owner):
+        return pltpu.make_async_remote_copy(
+            src_ref=prefix.at[place], dst_ref=prefix.at[place],
+            send_sem=prefix_send.at[to], recv_sem=prefix_recv.at[owner],
+            device_id={"tm": group + to}, device_id_type=MESH,
+        )
+
+    @pl.loop(0, group)
+    def _(to):
+        @pl.when(to > place)
+        def _():
+            pl.semaphore_wait(ready.at[side * group + to], 1)
+            half_copy(to, place).start()
+
+    @pl.when(side == 0)
+    def _():
+        @pl.loop(0, group)
+        def _(to):
+            pl.semaphore_wait(ready.at[group + to], 1)
+            part_copy(to, place).start()
+
+    def z_copy(ref, which, d):
+        return pltpu.make_async_remote_copy(
+            src_ref=ref.at[mine_z, :], dst_ref=ref.at[mine_z, :],
+            send_sem=z_send.at[which, d], recv_sem=z_recv.at[which, d],
+            device_id={"tm": lax.rem(zed + d, slices)}, device_id_type=MESH,
+        )
+
+    def z_start(ref, which):
+        @pl.loop(1, slices)
+        def _(d):
+            @pl.when(zed + d < slices)
+            def _():
+                z_copy(ref, which, d).start()
+
+    def z_arrive(ref, which):
+        @pl.loop(1, slices)
+        def _(d):
+            @pl.when(zed >= d)
+            def _():
+                z_copy(ref, which, d).wait_recv()
+
+    def z_sent(ref, which):
+        @pl.loop(1, slices)
+        def _(d):
+            @pl.when(zed + d < slices)
+            def _():
+                z_copy(ref, which, d).wait_send()
+
     blank = jnp.zeros((LINES * TERM, LANES), F32)
     far0[mine_z, :] = jnp.transpose(jnp.concatenate([spread0, blank], axis=0))[:COLS]
-    z_start(far0, 1)
+    z_start(far0, 0)
 
     half = LINES * TERM
     effect = jnp.concatenate(
@@ -273,17 +330,49 @@
         fars.append(unpacked(far * weight))
     spread = jnp.concatenate(fars, axis=0)
     far1[mine_z, :] = jnp.transpose(spread)[:COLS]
-    z_start(far1, 2)
-
-    z_arrive(ends_in, 0)
-
-    def one(i, state):
-        return slope * state + ends_in[pl.ds(pl.multiple_of(i * COLS, COLS), COLS), :]
-
-    plain = lax.fori_loop(0, zed + 1, one, jnp.zeros((COLS, NODES), F32))
-
-    z_arrive(far0, 1)
-    z_arrive(far1, 2)
+    z_start(far1, 1)
+
+    @pl.when(side == 1)
+    def _():
+        @pl.loop(0, group)
+        def _(sender):
+            part_copy(sender, sender).wait_recv()
+
+        bend = decay[:, pl.ds(pl.multiple_of(place * width, LANES), width)]
+        state = parts_in[0]
+        for k in range(1, group):
+            state = bend * state + parts_in[k]
+        prefix[place] = state
+
+        @pl.loop(0, group)
+        def _(to):
+            @pl.when(to != place)
+            def _():
+                prefix_copy(to, place).start()
+
+    @pl.loop(0, group)
+    def _(sender):
+        @pl.when(sender < place)
+        def _():
+            half_copy(sender, sender).wait_recv()
+
+    @pl.when(side == 1)
+    def _():
+        @pl.loop(0, group)
+        def _(owner):
+            @pl.when(owner != place)
+            def _():
+                prefix_copy(owner, owner).wait_recv()
+
+    bends = [slope[:, k * width : (k + 1) * width] for k in range(group)]
+
+    def one(i, states):
+        return tuple(bends[k] * states[k] + half_in[i, k] for k in range(group))
+
+    plain = lax.fori_loop(0, place + 1, one, tuple(prefix[k] for k in range(group)))
+
+    z_arrive(far0, 0)
+    z_arrive(far1, 1)
     high, low = split(jnp.concatenate([far0[...], far1[...]], axis=1))
     count = slices * COLS
     y = dot(jnp.concatenate([high, low], axis=0), m_high[...])
@@ -291,17 +380,40 @@
     state = jnp.zeros((COLS, NODES), F32)
     for i in range(slices):
         state = jnp.where(i <= zed, slope * state + y[i * COLS : (i + 1) * COLS], state)
-    out_ref[...] = plain + state
+    for k in range(group):
+        part = slice(k * width, (k + 1) * width)
+        out_ref[:, part] = plain[k] + state[:, part]
 
     all_of(near0, send_sems.at[0], recv0).wait_send()
     all_of(near12, send_sems.at[1], recv12).wait_send()
-    z_sent(ends_in, 0)
-    z_sent(far0, 1)
-    z_sent(far1, 2)
+
+    @pl.loop(0, group)
+    def _(to):
+        @pl.when(to > place)
+        def _():
+            half_copy(to, place).wait_send()
+
+    @pl.when(side == 0)
+    def _():
+        @pl.loop(0, group)
+        def _(to):
+            part_copy(to, place).wait_send()
+
+    @pl.when(side == 1)
+    def _():
+        @pl.loop(0, group)
+        def _(to):
+            @pl.when(to != place)
+            def _():
+                prefix_copy(to, place).wait_send()
+
+    z_sent(far0, 0)
+    z_sent(far1, 1)
 
 
 def shards(slices, subs, starts, inverses, retain, sources, decay, admittance, partner, delay, live, block):
     vmem, smem = pltpu.VMEM, pltpu.SMEM
+    group = slices // 2
     out = pl.pallas_call(
         functools.partial(kernel, slices, subs),
         out_shape=jax.ShapeDtypeStruct((COLS, NODES), F32),
@@ -318,11 +430,17 @@
             vmem((2 * LANES, NODES), BF16), vmem((2 * LANES, NODES), BF16),
             vmem((3, LINES * TERM, LANES), F32),
             vmem((subs, LINES, LANES), F32), vmem((subs, 2, LINES, LANES), F32),
-            vmem((slices * COLS, NODES), F32),
+            vmem((group, COLS, NODES // group), F32), vmem((group, COLS, NODES // group), F32),
+            vmem((group, group, COLS, NODES // group), F32),
+            vmem((group, COLS, NODES // group), F32),
             vmem((slices * COLS, LANES), F32), vmem((slices * COLS, LANES), F32),
             pltpu.SemaphoreType.DMA((9,)), pltpu.SemaphoreType.DMA((CHUNKS,)),
             pltpu.SemaphoreType.DMA((2,)), pltpu.SemaphoreType.DMA, pltpu.SemaphoreType.DMA,
-            pltpu.SemaphoreType.DMA((3, slices)), pltpu.SemaphoreType.DMA((3, slices)),
+            pltpu.SemaphoreType.DMA((2, slices)), pltpu.SemaphoreType.DMA((2, slices)),
+            pltpu.SemaphoreType.DMA((group,)), pltpu.SemaphoreType.DMA((group,)),
+            pltpu.SemaphoreType.DMA((group,)), pltpu.SemaphoreType.DMA((group,)),
+            pltpu.SemaphoreType.DMA((group,)), pltpu.SemaphoreType.DMA((group,)),
+            pltpu.SemaphoreType.REGULAR((slices,)),
         ],
         compiler_params=pltpu.CompilerParams(
             collective_id=0, has_side_effects=True, vmem_limit_bytes=67043328

time: 31.6 us -> 29.5 us (0.934)
  the two profiles are of different devices: /device:TPU:192 before, /device:TPU:128 now
where the time goes in v4:
time: 29.5 us; the launch traced here: 29.3 us
  Pallas kernels  27.9 us (95%)
  local copies, waits for them, and re-layouts  1.47 us (5%)
    pallas_call x1, Pallas kernels, shards(): pl.pallas_call(functools.partial(kernel, slices, subs), out_shape=jax.Sha...  27.9 us
    unnamed x1, local copies, waits for them, and re-layouts  1.47 us

profile of v4, /device:TPU:128, one launch (start us, length us, event | category | flops | bytes accessed | tf_op | source)
XLA Modules:
  0.0 29.3 jit_solution(5894535613584246945)
XLA Ops:
  0.0 27.9 %shard_map.100 = f32[16,1024]{1,0:T(8,128)} custom-call(f32[16,1024]{1,0:T(8,128)} %bitcast.6, f32[1024,1024]{1,0:T(8,128)} %bitcast.4, f32[1,1024]{1,0:T(1,128)} %retain_h.1, f32[16,1024]{1,0:T(8,128)} %bitcast.7, f32[1,1024]{1,0:T(1,128)} %decay_h.1, f32[1,8]{1,0:T(1,128)} %admittance_h.1, s32[1,8]{1,0:T(1,128)} %partner_h.1, s32[1,8]{1,0:T(1,128)} %delay_h.1, ...), custom_call_target="tpu_custom_call" | custom-call | tf_op jit(solution)/shard_map/pallas_call | solution.py:417
  27.9 1.5 %copy.12 = f32[1,1,16,1024]{3,2,1,0:T(8,128)} copy(f32[1,1,16,1024]{3,2,1,0:T(8,128)} %bitcast.5) | data formatting | bytes 131072

commit v5 on v4

--- a/solution.py
+++ b/solution.py
@@ -52,9 +52,9 @@
     out_ref,
     starts, sources, retain, decay, admittance, partner, delay, live, block,
     raw, a_high, a_low, z_all, z_turned, z_both, m_high, m_low,
-    rows, near0, near12, offset, parts_in, half_in, prefix, far0, far1,
+    rows, near0, near12, offset, parts_in, half_in, sums, plain, far0, far1,
     in_sems, raw_sems, send_sems, recv0, recv12, z_send, z_recv,
-    part_send, part_recv, half_send, half_recv, prefix_send, prefix_recv, ready,
+    part_send, part_recv, half_send, half_recv, sum_send, sum_recv, ready,
 ):
     group = slices // 2
     zed = lax.axis_index("tm")
@@ -62,7 +62,7 @@
 
     far0[...] = jnp.zeros_like(far0)
     far1[...] = jnp.zeros_like(far1)
-    prefix[...] = jnp.zeros_like(prefix)
+    plain[...] = jnp.zeros_like(plain)
 
     pairs = (
         (starts_h, starts), (block_h, block), (retain_h, retain), (sources_h, sources),
@@ -236,6 +236,7 @@
     side = lax.div(zed, group)
     place = lax.rem(zed, group)
     half_in[place] = offset[...]
+    parts_in[zed] = offset[place]
 
     def half_copy(to, sender):
         return pltpu.make_async_remote_copy(
@@ -246,31 +247,36 @@
 
     def part_copy(to, sender):
         return pltpu.make_async_remote_copy(
-            src_ref=offset.at[to], dst_ref=parts_in.at[place],
+            src_ref=offset.at[to], dst_ref=parts_in.at[zed],
             send_sem=part_send.at[to], recv_sem=part_recv.at[sender],
             device_id={"tm": group + to}, device_id_type=MESH,
         )
 
-    def prefix_copy(to, owner):
-        return pltpu.make_async_remote_copy(
-            src_ref=prefix.at[place], dst_ref=prefix.at[place],
-            send_sem=prefix_send.at[to], recv_sem=prefix_recv.at[owner],
+    def sum_copy(to, owner):
+        return pltpu.make_async_remote_copy(
+            src_ref=sums.at[to], dst_ref=plain.at[place],
+            send_sem=sum_send.at[to], recv_sem=sum_recv.at[owner],
             device_id={"tm": group + to}, device_id_type=MESH,
         )
 
     @pl.loop(0, group)
     def _(to):
-        @pl.when(to > place)
-        def _():
-            pl.semaphore_wait(ready.at[side * group + to], 1)
-            half_copy(to, place).start()
+        @pl.when(zed < group + to)
+        def _():
+            pl.semaphore_wait(ready.at[group + to], 1)
+
+        @pl.when(zed != group + to)
+        def _():
+            part_copy(to, zed).start()
 
     @pl.when(side == 0)
     def _():
         @pl.loop(0, group)
         def _(to):
-            pl.semaphore_wait(ready.at[group + to], 1)
-            part_copy(to, place).start()
+            @pl.when(to > place)
+            def _():
+                pl.semaphore_wait(ready.at[to], 1)
+                half_copy(to, place).start()
 
     def z_copy(ref, which, d):
         return pltpu.make_async_remote_copy(
@@ -334,42 +340,47 @@
 
     @pl.when(side == 1)
     def _():
-        @pl.loop(0, group)
+        @pl.loop(0, slices)
         def _(sender):
-            part_copy(sender, sender).wait_recv()
+            @pl.when(sender != zed)
+            def _():
+                part_copy(place, sender).wait_recv()
 
         bend = decay[:, pl.ds(pl.multiple_of(place * width, LANES), width)]
         state = parts_in[0]
-        for k in range(1, group):
+        for k in range(1, slices):
             state = bend * state + parts_in[k]
-        prefix[place] = state
+            if k >= group:
+                sums[k - group] = state
+        plain[place] = sums[place]
 
         @pl.loop(0, group)
         def _(to):
             @pl.when(to != place)
             def _():
-                prefix_copy(to, place).start()
-
-    @pl.loop(0, group)
-    def _(sender):
-        @pl.when(sender < place)
-        def _():
-            half_copy(sender, sender).wait_recv()
-
-    @pl.when(side == 1)
-    def _():
+                sum_copy(to, place).start()
+
         @pl.loop(0, group)
         def _(owner):
             @pl.when(owner != place)
             def _():
-                prefix_copy(owner, owner).wait_recv()
+                sum_copy(owner, owner).wait_recv()
+
+    @pl.when(side == 0)
+    def _():
+        @pl.loop(0, group)
+        def _(sender):
+            @pl.when(sender < place)
+            def _():
+                half_copy(sender, sender).wait_recv()
 
     bends = [slope[:, k * width : (k + 1) * width] for k in range(group)]
 
     def one(i, states):
         return tuple(bends[k] * states[k] + half_in[i, k] for k in range(group))
 
-    plain = lax.fori_loop(0, place + 1, one, tuple(prefix[k] for k in range(group)))
+    steps = jnp.where(side == 0, place + 1, 0)
+    summed = lax.fori_loop(0, steps, one, tuple(plain[k] for k in range(group)))
 
     z_arrive(far0, 0)
     z_arrive(far1, 1)
@@ -382,30 +393,24 @@
         state = jnp.where(i <= zed, slope * state + y[i * COLS : (i + 1) * COLS], state)
     for k in range(group):
         part = slice(k * width, (k + 1) * width)
-        out_ref[:, part] = plain[k] + state[:, part]
+        out_ref[:, part] = summed[k] + state[:, part]
 
     all_of(near0, send_sems.at[0], recv0).wait_send()
     all_of(near12, send_sems.at[1], recv12).wait_send()
 
     @pl.loop(0, group)
     def _(to):
-        @pl.when(to > place)
+        @pl.when(zed != group + to)
+        def _():
+            part_copy(to, zed).wait_send()
+
+        @pl.when((side == 0) & (to > place))
         def _():
             half_copy(to, place).wait_send()
 
-    @pl.when(side == 0)
-    def _():
-        @pl.loop(0, group)
-        def _(to):
-            part_copy(to, place).wait_send()
-
-    @pl.when(side == 1)
-    def _():
-        @pl.loop(0, group)
-        def _(to):
-            @pl.when(to != place)
-            def _():
-                prefix_copy(to, place).wait_send()
+        @pl.when((side == 1) & (to != place))
+        def _():
+            sum_copy(to, place).wait_send()
 
     z_sent(far0, 0)
     z_sent(far1, 1)
@@ -430,25 +435,25 @@
             vmem((2 * LANES, NODES), BF16), vmem((2 * LANES, NODES), BF16),
             vmem((3, LINES * TERM, LANES), F32),
             vmem((subs, LINES, LANES), F32), vmem((subs, 2, LINES, LANES), F32),
+            vmem((group, COLS, NODES // group), F32), vmem((slices, COLS, NODES // group), F32),
+            vmem((group, group, COLS, NODES // group), F32),
             vmem((group, COLS, NODES // group), F32), vmem((group, COLS, NODES // group), F32),
-            vmem((group, group, COLS, NODES // group), F32),
-            vmem((group, COLS, NODES // group), F32),
             vmem((slices * COLS, LANES), F32), vmem((slices * COLS, LANES), F32),
             pltpu.SemaphoreType.DMA((9,)), pltpu.SemaphoreType.DMA((CHUNKS,)),
             pltpu.SemaphoreType.DMA((2,)), pltpu.SemaphoreType.DMA, pltpu.SemaphoreType.DMA,
             pltpu.SemaphoreType.DMA((2, slices)), pltpu.SemaphoreType.DMA((2, slices)),
-            pltpu.SemaphoreType.DMA((group,)), pltpu.SemaphoreType.DMA((group,)),
+            pltpu.SemaphoreType.DMA((group,)), pltpu.SemaphoreType.DMA((slices,)),
             pltpu.SemaphoreType.DMA((group,)), pltpu.SemaphoreType.DMA((group,)),
             pltpu.SemaphoreType.DMA((group,)), pltpu.SemaphoreType.DMA((group,)),
             pltpu.SemaphoreType.REGULAR((slices,)),
         ],
         compiler_params=pltpu.CompilerParams(
-            collective_id=0, has_side_effects=True, vmem_limit_bytes=67043328
+            collective_id=0, has_side_effects=True, vmem_limit_bytes=48 * 1024 * 1024
         ),
-    )(
+    )(*[pltpu.with_memory_space_constraint(a, pltpu.HBM) for a in (
         starts.reshape(COLS, NODES), inverses.reshape(NODES, NODES), retain,
         sources.reshape(COLS, NODES), decay, admittance, partner, delay, live, block,
-    )
+    )])
     return out.reshape(1, 1, COLS, NODES)
 
 

time: 29.5 us -> 25.1 us (0.85)
  the two profiles are of different devices: /device:TPU:128 before, /device:TPU:192 now
where the time goes in v5:
time: 25.1 us; the launch traced here: 25 us
  Pallas kernels  24.4 us (97%)
  local copies, waits for them, and re-layouts  0.63 us (3%)
    pallas_call x1, Pallas kernels, shards(): pl.pallas_call(functools.partial(kernel, slices, subs), out_shape=jax.Sha...  24.4 us
    unnamed x1, local copies, waits for them, and re-layouts  0.63 us

profile of v5, /device:TPU:192, one launch (start us, length us, event | category | flops | bytes accessed | tf_op | source)
XLA Modules:
  0.0 25.0 jit_solution(16449453589888495418)
XLA Ops:
  0.0 24.4 %shard_map.100 = f32[16,1024]{1,0:T(8,128)S(1)} custom-call(f32[16,1024]{1,0:T(8,128)} %bitcast.6, f32[1024,1024]{1,0:T(8,128)} %bitcast.5, f32[1,1024]{1,0:T(1,128)} %retain_h.1, f32[16,1024]{1,0:T(8,128)} %bitcast.7, f32[1,1024]{1,0:T(1,128)} %decay_h.1, f32[1,8]{1,0:T(1,128)} %admittance_h.1, s32[1,8]{1,0:T(1,128)} %partner_h.1, s32[1,8]{1,0:T(1,128)} %delay_h.1, ...), custom_call_target="tpu_custom_call" | custom-call | tf_op jit(solution)/shard_map/pallas_call | solution.py:422
  24.4 0.6 %copy.12 = f32[1,1,16,1024]{3,2,1,0:T(8,128)} copy(f32[1,1,16,1024]{3,2,1,0:T(8,128)S(1)} %bitcast.4) | data formatting | bytes 131072

commit v6 on v5

--- a/solution.py
+++ b/solution.py
@@ -43,6 +43,25 @@
     return jnp.concatenate(
         [far] + [pltpu.roll(far, LANES - COLS * t, 1) for t in range(1, TERM)], axis=0
     )
+
+
+def far_first(me, subs):
+    if subs != 32:
+        return [lax.rem(me + o, subs) for o in range(1, subs)]
+    rows = [8 * ((lax.div(me, 8) + d) & 3) for d in range(4)]
+    columns = [2 * ((lax.div(me, 2) + d) & 3) for d in range(4)]
+    cores = [(me + d) & 1 for d in range(2)]
+    apart = [(y, x, core) for core in range(2) for y in range(4) for x in range(4)][1:]
+    hops = lambda d: min(d, 4 - d)
+    apart.sort(key=lambda d: -(hops(d[0]) + hops(d[1])))
+    return [rows[y] + columns[x] + cores[core] for y, x, core in apart]
+
+
+def hops_of(me, subs):
+    if subs != 32:
+        return me
+    row, column = lax.div(me, 8) & 3, lax.div(me, 2) & 3
+    return jnp.minimum(row, 4 - row) + jnp.minimum(column, 4 - column)
 
 
 def kernel(
@@ -84,11 +103,9 @@
         chunk.start()
     barrier = pltpu.get_barrier_semaphore()
 
-    @pl.loop(1, subs)
-    def _(o):
-        pl.semaphore_signal(
-            barrier, inc=1, device_id={"sub": lax.rem(me + o, subs)}, device_id_type=MESH
-        )
+    others = far_first(me, subs)
+    for other in others:
+        pl.semaphore_signal(barrier, inc=1, device_id={"sub": other}, device_id_type=MESH)
 
     @pl.loop(1, slices)
     def _(o):
@@ -129,7 +146,55 @@
     pick(0)
     near0[me] = packed(rows, 0, 0)
 
+    high, low = split(turned)
+    z_both[:, :LANES] = high
+    z_both[:, LANES:] = low
+
+    def divide():
+        for k in range(CHUNKS):
+            chunks[k].wait()
+            piece = pl.ds(k * depth, depth)
+            high, low = split(raw[piece, :] * gain)
+            a_high[piece, :] = high
+            a_low[piece, :] = low
+
+    def advance(k, carry):
+        both = z_both[...]
+        y = dot(a_high[...], both) + dot(a_low[...], both)
+        new = y[:, :LANES] + y[:, LANES:]
+        z_all[k] = new.reshape(NODES // TERM, TERM, LANES)
+        high, low = split(new)
+        z_both[:, :LANES] = high
+        z_both[:, LANES:] = low
+        z_turned[k - 1] = jnp.transpose(new)
+        return carry
+
+    hops = hops_of(me, subs)
+    ahead = jnp.maximum(1 - hops, 0)
+
+    @pl.when(hops < 4)
+    def _():
+        divide()
+
+    lax.fori_loop(1, 1 + ahead, advance, 0)
+
     pl.semaphore_wait(barrier, subs - 1 + zed)
+
+    def sub_copy(ref, send, recv, other):
+        return pltpu.make_async_remote_copy(
+            src_ref=ref.at[me], dst_ref=ref.at[me], send_sem=send, recv_sem=recv,
+            device_id={"sub": other}, device_id_type=MESH,
+        )
+
+    def all_of(ref, send, recv):
+        whole = ref.at[pl.ds(0, subs - 1)]
+        return pltpu.make_async_remote_copy(
+            src_ref=whole, dst_ref=whole, send_sem=send, recv_sem=recv,
+            device_id={"sub": lax.rem(me + 1, subs)}, device_id_type=MESH,
+        )
+
+    for other in others:
+        sub_copy(near0, send_sems.at[0], recv0, other).start()
 
     @pl.loop(1, slices)
     def _(o):
@@ -140,52 +205,104 @@
                 device_id_type=MESH,
             )
 
-    def sub_copy(ref, send, recv, o):
-        return pltpu.make_async_remote_copy(
-            src_ref=ref.at[me], dst_ref=ref.at[me], send_sem=send, recv_sem=recv,
-            device_id={"sub": lax.rem(me + o, subs)}, device_id_type=MESH,
-        )
-
-    def all_of(ref, send, recv):
-        whole = ref.at[pl.ds(0, subs - 1)]
-        return pltpu.make_async_remote_copy(
-            src_ref=whole, dst_ref=whole, send_sem=send, recv_sem=recv,
-            device_id={"sub": lax.rem(me + 1, subs)}, device_id_type=MESH,
-        )
-
-    @pl.loop(1, subs)
-    def _(o):
-        sub_copy(near0, send_sems.at[0], recv0, o).start()
-
     slot8 = lax.broadcasted_iota(jnp.int32, (LINES, LANES), 0)
     weight = jnp.zeros((LINES, LANES), F32)
     for l in range(LINES):
         weight = jnp.where(slot8 == l, admittance[0, l] * live[0, l].astype(F32), weight)
     weight = weight * packed(rows, 0, 3 * COLS)
 
-    high, low = split(turned)
-    z_both[:, :LANES] = high
-    z_both[:, LANES:] = low
-    for k in range(CHUNKS):
-        chunks[k].wait()
-        piece = pl.ds(k * depth, depth)
-        high, low = split(raw[piece, :] * gain)
-        a_high[piece, :] = high
-        a_low[piece, :] = low
-
-    def advance(k):
-        both = z_both[...]
-        y = dot(a_high[...], both) + dot(a_low[...], both)
-        new = y[:, :LANES] + y[:, LANES:]
-        z_all[k] = new.reshape(NODES // TERM, TERM, LANES)
-        high, low = split(new)
-        z_both[:, :LANES] = high
-        z_both[:, LANES:] = low
-        z_turned[k - 1] = jnp.transpose(new)
-
-    @pl.loop(1, 4)
-    def _(k):
-        advance(k)
+    @pl.when(hops >= 4)
+    def _():
+        divide()
+
+    lax.fori_loop(1 + ahead, 5, advance, 0)
+
+    mine_z = pl.ds(pl.multiple_of(zed * COLS, COLS), COLS)
+    base = z_turned[3, :COLS, :]
+    for k in range(4):
+        base = base + z_turned[k, COLS : 2 * COLS, :]
+    slope = decay[...]
+    base = jnp.where(zed == 0, base, base - slope * starts[...])
+    width = NODES // group
+    for k in range(group):
+        offset[k] = base[:, k * width : (k + 1) * width]
+    side = lax.div(zed, group)
+    place = lax.rem(zed, group)
+    half_in[place] = offset[...]
+    parts_in[zed] = offset[place]
+
+    def half_copy(to, sender):
+        return pltpu.make_async_remote_copy(
+            src_ref=offset, dst_ref=half_in.at[place],
+            send_sem=half_send.at[to], recv_sem=half_recv.at[sender],
+            device_id={"tm": side * group + to}, device_id_type=MESH,
+        )
+
+    def part_copy(to, sender):
+        return pltpu.make_async_remote_copy(
+            src_ref=offset.at[to], dst_ref=parts_in.at[zed],
+            send_sem=part_send.at[to], recv_sem=part_recv.at[sender],
+            device_id={"tm": group + to}, device_id_type=MESH,
+        )
+
+    def sum_copy(to, owner):
+        return pltpu.make_async_remote_copy(
+            src_ref=sums.at[to], dst_ref=plain.at[place],
+            send_sem=sum_send.at[to], recv_sem=sum_recv.at[owner],
+            device_id={"tm": group + to}, device_id_type=MESH,
+        )
+
+    def send_offsets():
+        @pl.loop(0, group)
+        def _(to):
+            @pl.when(zed < group + to)
+            def _():
+                pl.semaphore_wait(ready.at[group + to], 1)
+
+            @pl.when(zed != group + to)
+            def _():
+                part_copy(to, zed).start()
+
+        @pl.when(side == 0)
+        def _():
+            @pl.loop(0, group)
+            def _(to):
+                @pl.when(to > place)
+                def _():
+                    pl.semaphore_wait(ready.at[to], 1)
+                    half_copy(to, place).start()
+
+    @pl.when(zed >= 2)
+    def _():
+        send_offsets()
+
+    def z_copy(ref, which, d):
+        return pltpu.make_async_remote_copy(
+            src_ref=ref.at[mine_z, :], dst_ref=ref.at[mine_z, :],
+            send_sem=z_send.at[which, d], recv_sem=z_recv.at[which, d],
+            device_id={"tm": lax.rem(zed + d, slices)}, device_id_type=MESH,
+        )
+
+    def z_start(ref, which):
+        @pl.loop(1, slices)
+        def _(d):
+            @pl.when(zed + d < slices)
+            def _():
+                z_copy(ref, which, d).start()
+
+    def z_arrive(ref, which):
+        @pl.loop(1, slices)
+        def _(d):
+            @pl.when(zed >= d)
+            def _():
+                z_copy(ref, which, d).wait_recv()
+
+    def z_sent(ref, which):
+        @pl.loop(1, slices)
+        def _(d):
+            @pl.when(zed + d < slices)
+            def _():
+                z_copy(ref, which, d).wait_send()
 
     pick(1)
     pick(2)
@@ -218,93 +335,12 @@
     near12[me, 0] = packed(rows, 1, 0)
     near12[me, 1] = packed(rows, 2, 0)
 
-    @pl.loop(1, subs)
-    def _(o):
-        sub_copy(near12, send_sems.at[1], recv12, o).start()
-
-    advance(4)
-
-    mine_z = pl.ds(pl.multiple_of(zed * COLS, COLS), COLS)
-    base = z_turned[3, :COLS, :]
-    for k in range(4):
-        base = base + z_turned[k, COLS : 2 * COLS, :]
-    slope = decay[...]
-    base = jnp.where(zed == 0, base, base - slope * starts[...])
-    width = NODES // group
-    for k in range(group):
-        offset[k] = base[:, k * width : (k + 1) * width]
-    side = lax.div(zed, group)
-    place = lax.rem(zed, group)
-    half_in[place] = offset[...]
-    parts_in[zed] = offset[place]
-
-    def half_copy(to, sender):
-        return pltpu.make_async_remote_copy(
-            src_ref=offset, dst_ref=half_in.at[place],
-            send_sem=half_send.at[to], recv_sem=half_recv.at[sender],
-            device_id={"tm": side * group + to}, device_id_type=MESH,
-        )
-
-    def part_copy(to, sender):
-        return pltpu.make_async_remote_copy(
-            src_ref=offset.at[to], dst_ref=parts_in.at[zed],
-            send_sem=part_send.at[to], recv_sem=part_recv.at[sender],
-            device_id={"tm": group + to}, device_id_type=MESH,
-        )
-
-    def sum_copy(to, owner):
-        return pltpu.make_async_remote_copy(
-            src_ref=sums.at[to], dst_ref=plain.at[place],
-            send_sem=sum_send.at[to], recv_sem=sum_recv.at[owner],
-            device_id={"tm": group + to}, device_id_type=MESH,
-        )
-
-    @pl.loop(0, group)
-    def _(to):
-        @pl.when(zed < group + to)
-        def _():
-            pl.semaphore_wait(ready.at[group + to], 1)
-
-        @pl.when(zed != group + to)
-        def _():
-            part_copy(to, zed).start()
-
-    @pl.when(side == 0)
+    for other in others:
+        sub_copy(near12, send_sems.at[1], recv12, other).start()
+
+    @pl.when(zed < 2)
     def _():
-        @pl.loop(0, group)
-        def _(to):
-            @pl.when(to > place)
-            def _():
-                pl.semaphore_wait(ready.at[to], 1)
-                half_copy(to, place).start()
-
-    def z_copy(ref, which, d):
-        return pltpu.make_async_remote_copy(
-            src_ref=ref.at[mine_z, :], dst_ref=ref.at[mine_z, :],
-            send_sem=z_send.at[which, d], recv_sem=z_recv.at[which, d],
-            device_id={"tm": lax.rem(zed + d, slices)}, device_id_type=MESH,
-        )
-
-    def z_start(ref, which):
-        @pl.loop(1, slices)
-        def _(d):
-            @pl.when(zed + d < slices)
-            def _():
-                z_copy(ref, which, d).start()
-
-    def z_arrive(ref, which):
-        @pl.loop(1, slices)
-        def _(d):
-            @pl.when(zed >= d)
-            def _():
-                z_copy(ref, which, d).wait_recv()
-
-    def z_sent(ref, which):
-        @pl.loop(1, slices)
-        def _(d):
-            @pl.when(zed + d < slices)
-            def _():
-                z_copy(ref, which, d).wait_send()
+        send_offsets()
 
     blank = jnp.zeros((LINES * TERM, LANES), F32)
     far0[mine_z, :] = jnp.transpose(jnp.concatenate([spread0, blank], axis=0))[:COLS]

time: 25.1 us -> 24.2 us (0.964)
  the two profiles are of different devices: /device:TPU:192 before, /device:TPU:224 now
where the time goes in v6:
time: 24.2 us
  Pallas kernels  23.5 us (97%)
  local copies, waits for them, and re-layouts  0.63 us (3%)
    pallas_call x1, Pallas kernels, shards(): pl.pallas_call(functools.partial(kernel, slices, subs), out_shape=jax.Sha...  23.5 us
    unnamed x1, local copies, waits for them, and re-layouts  0.63 us

profile of v6, /device:TPU:224, one launch (start us, length us, event | category | flops | bytes accessed | tf_op | source)
XLA Modules:
  0.0 24.2 jit_solution(17061162798282546847)
XLA Ops:
  0.0 23.5 %shard_map.100 = f32[16,1024]{1,0:T(8,128)S(1)} custom-call(f32[16,1024]{1,0:T(8,128)} %bitcast.6, f32[1024,1024]{1,0:T(8,128)} %bitcast.5, f32[1,1024]{1,0:T(1,128)} %retain_h.1, f32[16,1024]{1,0:T(8,128)} %bitcast.7, f32[1,1024]{1,0:T(1,128)} %decay_h.1, f32[1,8]{1,0:T(1,128)} %admittance_h.1, s32[1,8]{1,0:T(1,128)} %partner_h.1, s32[1,8]{1,0:T(1,128)} %delay_h.1, ...), custom_call_target="tpu_custom_call" | custom-call | tf_op jit(solution)/shard_map/pallas_call | solution.py:458
  23.5 0.6 %copy.12 = f32[1,1,16,1024]{3,2,1,0:T(8,128)} copy(f32[1,1,16,1024]{3,2,1,0:T(8,128)S(1)} %bitcast.4) | data formatting | bytes 131072

commit v7 on v6

--- a/solution.py
+++ b/solution.py
@@ -360,6 +360,28 @@
     m_high[...] = high
     m_low[...] = low
 
+    @pl.when(side == 1)
+    def _():
+        @pl.loop(0, slices)
+        def _(sender):
+            @pl.when(sender != zed)
+            def _():
+                part_copy(place, sender).wait_recv()
+
+        bend = decay[:, pl.ds(pl.multiple_of(place * width, LANES), width)]
+        state = parts_in[0]
+        for k in range(1, slices):
+            state = bend * state + parts_in[k]
+            if k >= group:
+                sums[k - group] = state
+        plain[place] = sums[place]
+
+        @pl.loop(0, group)
+        def _(to):
+            @pl.when(to != place)
+            def _():
+                sum_copy(to, place).start()
+
     all_of(near12, send_sems.at[1], recv12).wait_recv()
     fars = []
     for step in (2, 3):
@@ -376,26 +398,6 @@
 
     @pl.when(side == 1)
     def _():
-        @pl.loop(0, slices)
-        def _(sender):
-            @pl.when(sender != zed)
-            def _():
-                part_copy(place, sender).wait_recv()
-
-        bend = decay[:, pl.ds(pl.multiple_of(place * width, LANES), width)]
-        state = parts_in[0]
-        for k in range(1, slices):
-            state = bend * state + parts_in[k]
-            if k >= group:
-                sums[k - group] = state
-        plain[place] = sums[place]
-
-        @pl.loop(0, group)
-        def _(to):
-            @pl.when(to != place)
-            def _():
-                sum_copy(to, place).start()
-
         @pl.loop(0, group)
         def _(owner):
             @pl.when(owner != place)

time: 24.2 us -> 23.4 us (0.967)
  the two profiles are of different devices: /device:TPU:224 before, /device:TPU:192 now
where the time goes in v7:
time: 23.4 us; the launch traced here: 23.3 us
  Pallas kernels  22.6 us (97%)
  local copies, waits for them, and re-layouts  0.63 us (3%)
    pallas_call x1, Pallas kernels, shards(): pl.pallas_call(functools.partial(kernel, slices, subs), out_shape=jax.Sha...  22.6 us
    unnamed x1, local copies, waits for them, and re-layouts  0.63 us

profile of v7, /device:TPU:192, one launch (start us, length us, event | category | flops | bytes accessed | tf_op | source)
XLA Modules:
  0.0 23.3 jit_solution(17197456991437156176)
XLA Ops:
  0.0 22.6 %shard_map.100 = f32[16,1024]{1,0:T(8,128)S(1)} custom-call(f32[16,1024]{1,0:T(8,128)} %bitcast.6, f32[1024,1024]{1,0:T(8,128)} %bitcast.5, f32[1,1024]{1,0:T(1,128)} %retain_h.1, f32[16,1024]{1,0:T(8,128)} %bitcast.7, f32[1,1024]{1,0:T(1,128)} %decay_h.1, f32[1,8]{1,0:T(1,128)} %admittance_h.1, s32[1,8]{1,0:T(1,128)} %partner_h.1, s32[1,8]{1,0:T(1,128)} %delay_h.1, ...), custom_call_target="tpu_custom_call" | custom-call | tf_op jit(solution)/shard_map/pallas_call | solution.py:460
  22.7 0.6 %copy.12 = f32[1,1,16,1024]{3,2,1,0:T(8,128)} copy(f32[1,1,16,1024]{3,2,1,0:T(8,128)S(1)} %bitcast.4) | data formatting | bytes 131072
